TPU v7x, 128 devices: a whole 4x4x4 slice. The times are simulated.
128 devices in a mesh: node: 128 (over z, x, y, core).
Axes of the slice: x: 4, y: 4, z: 4, core: 2. Of those that a mesh axis runs over, the one named last changes fastest.
Arguments:
- labels: bfloat16 [524288, 512], P('node'), may hold values from -6 to 6
- seed_mask: int32 [524288], P('node'), may hold values 0 or 1
- band_w: bfloat16 [4096, 3, 128, 128], P('node'), may hold values from 0.0009994507 to 1
- far_block: int32 [128, 128, 2], P('node'), may hold values from 0 to 511
- far_tile: int32 [128, 128, 2], P('node'), may hold values from 0 to 31
- far_count: int32 [128, 128], P('node'), may hold values from 0 to 2, as said below
- far_w: bfloat16 [128, 128, 2, 8, 128], P('node'), may hold values from 0.049804688 to 2
Outputs:
- final_labels: bfloat16 [524288, 512], P('node')
- residual: float32 [2, 4096], P(None, 'node')
Inputs may be any that keep to these rules, and one draw needn't show every extreme that they name: `far_count`: in every draw at least one destination shard has all 2 slots live from every source shard; other counts vary from pair to pair.
All inputs are finite; a program needn't handle non-finite values. No bound on the sum of `seed_mask` on one device may be relied on, other than what follows from the above.
Results may differ from a plain program's by a relative error of at most 0.0027.
Values may be sent and summed in bfloat16 or wider, within the bound.
No kernel may reach another device: no remote copies, remote signals or barrier semaphores. Data moves between devices by JAX's collectives and lax.ppermute only.
A program may use at most 128 MiB of HBM per device.

v0:
```python
import jax
import jax.numpy as jnp
from jax import lax
from jax.sharding import PartitionSpec as P

ITERS = 2


def with_halo(block, sides, width):
    for axis, dim in sides:
        count = lax.axis_size(axis)
        forward = [(i, i + 1) for i in range(count - 1)]
        forward.append((count - 1, 0))
        backward = [(target, source) for source, target in forward]
        low = lax.ppermute(
            lax.slice_in_dim(block, block.shape[dim] - width, None, axis=dim), axis, forward
        )
        high = lax.ppermute(lax.slice_in_dim(block, 0, width, axis=dim), axis, backward)
        block = jnp.concatenate([low, block, high], axis=dim)
    return block


def fetch_blocks(current, requests, block_rows, classes):
    blocks = current.reshape(-1, block_rows, classes)[requests]
    return lax.all_to_all(blocks, "node", split_axis=0, concat_axis=0, tiled=True)


def cycle_tiles(current, tile_count, tile_rows, classes):
    tiles = current.reshape(tile_count, tile_rows, classes)
    return with_halo(tiles, (("node", 0),), 1)


def body(labels, seed_mask, band_w, far_block, far_tile, far_count, far_w):
    node_rows, classes = labels.shape
    tile_count = band_w.shape[0]
    tile_rows = band_w.shape[2]
    peer_count = far_w.shape[1]
    slot_count = far_w.shape[2]
    block_rows = far_w.shape[3]
    requests = lax.all_to_all(far_block, "node", split_axis=1, concat_axis=0, tiled=True).reshape(
        peer_count, slot_count
    )
    live_slots = jnp.arange(slot_count)[None, :] < far_count[0][:, None]
    weights = jnp.where(live_slots[:, :, None, None], far_w[0], jnp.zeros((), jnp.bfloat16))
    flat_tiles = far_tile[0].reshape(-1)
    weight_sums = jnp.sum(weights, axis=2, dtype=jnp.float32).reshape(-1, tile_rows)
    degree_far = jnp.zeros((tile_count, tile_rows), jnp.float32).at[flat_tiles].add(weight_sums)
    degree = jnp.sum(band_w, axis=(1, 3), dtype=jnp.float32) + degree_far
    slot_weights = weights.reshape(peer_count * slot_count, block_rows, tile_rows)
    onehot = jnp.arange(tile_count)[:, None] == flat_tiles[None, :]
    placed = jnp.where(onehot[:, :, None, None], slot_weights[None], jnp.zeros((), jnp.bfloat16))
    placed = placed.reshape(tile_count, peer_count * slot_count * block_rows, tile_rows)
    seeded = (seed_mask == 1).reshape(tile_count, tile_rows, 1)
    clamped = labels.astype(jnp.float32).reshape(tile_count, tile_rows, classes)
    current = labels
    residuals = []
    for sweep in range(ITERS):
        padded = cycle_tiles(current, tile_count, tile_rows, classes)
        received = fetch_blocks(current, requests, block_rows, classes)
        band_sum = jnp.zeros((tile_count, tile_rows, classes), jnp.float32)
        for offset in (-1, 0, 1):
            source = padded[1 + offset : 1 + offset + tile_count]
            band_sum = band_sum + jnp.einsum(
                "itr,irc->itc", band_w[:, offset + 1], source, preferred_element_type=jnp.float32
            )
        far_sum = jnp.einsum(
            "tqr,qc->trc", placed, received.reshape(-1, classes), preferred_element_type=jnp.float32
        )
        averaged = (band_sum + far_sum) / degree[:, :, None]
        row_scale = jnp.sqrt(jnp.mean(averaged * averaged, axis=2, keepdims=True))
        scaled = averaged / jnp.maximum(row_scale, 0.05)
        fresh = jnp.where(seeded, clamped, scaled).astype(jnp.bfloat16)
        previous = current.astype(jnp.float32).reshape(tile_count, tile_rows, classes)
        residuals.append(jnp.sum(jnp.abs(fresh.astype(jnp.float32) - previous), axis=(1, 2)))
        current = fresh.reshape(node_rows, classes)
    return (current, jnp.stack(residuals))


def solution(mesh):
    placed = (
        P("node", None),
        P("node"),
        P("node", None, None, None),
        P("node", None, None),
        P("node", None, None),
        P("node", None),
        P("node", None, None, None, None),
    )
    return jax.shard_map(
        body,
        mesh=mesh,
        in_specs=placed,
        out_specs=(P("node", None), P(None, "node")),
        check_vma=False,
    )
```

profile of v0, /device:TPU:0, one launch (start us, length us, event | category | flops | bytes accessed | tf_op | source)
XLA Modules:
  0.0 184.5 jit_solution(16199250453833278590)
XLA Ops:
  0.6 1.4 copy.27
  2.0 11.2 %all-to-all-start = ((s32[1,128,2]{2,0,1:T(1,128)}), s32[1,128,2]{2,0,1:T(1,128)S(1)}, u32[]{:S(2)}, u32[]{:S(2)}) async-start(s32[1,128,2]{2,0,1:T(1,128)} %copy.27), calls=%async_computation | async-start | bytes 131072 | tf_op jit(solution)/shard_map/all_to_all | solution.py:40
  14.2 7.1 %collective-permute-start.1 = (bf16[1,128,512]{2,1,0:T(8,128)(2,1)S(1)}, bf16[1,128,512]{2,1,0:T(8,128)(2,1)S(1)}, u32[]{:S(2)}, u32[]{:S(2)}) collective-permute-start(bf16[1,128,512]{2,1,0:T(8,128)(2,1)S(1)} %get-tuple-element.6), channel_id=1, source_target_pairs={{1,0},{2,1},{3,2},{4,3},{5,4},{6,5},{7,6},{8,7},{9,8},{10,9},{11,1... | collective-permute-start | bytes 393224 | tf_op jit(solution)/shard_map/ppermute | solution.py:18
  23.4 1.4 bitcast_select_fusion.1
  25.1 4.3 %gather_fusion = bf16[256,8,512]{2,1,0:T(8,128)(2,1)} fusion(bf16[512,8,512]{2,1,0:T(8,128)(2,1)} %bitcast.75, s32[1024]{0:T(1024)S(1)} %pad_clamp_fusion), kind=kCustom, calls=%fused_computation | custom fusion | bytes 4195328 | tf_op jit(solution)/shard_map/gather | solution.py:24
  29.4 9.6 %all-to-all-start.1 = ((bf16[128,2,8,512]{3,2,1,0:T(8,128)(2,1)}), bf16[128,2,8,512]{3,2,1,0:T(8,128)(2,1)}, u32[]{:S(2)}, u32[]{:S(2)}) async-start(bf16[128,2,8,512]{3,2,1,0:T(8,128)(2,1)} %bitcast.14), calls=%async_computation.1 | async-start | bytes 4194304 | tf_op jit(solution)/shard_map/all_to_all | solution.py:25
  40.4 2.5 %convert_reduce_fusion = f32[32,128]{1,0:T(8,128)S(1)} fusion(bf16[32,3,128,128]{3,2,1,0:T(8,128)(2,1)} %param.9), kind=kLoop, calls=%fused_computation.29 | loop fusion | flops 3141632 | bytes 3162112 | tf_op jit(solution)/shard_map/reduce_sum | solution.py:48
  42.9 2.1 %scatter_fusion = f32[32,128]{1,0:T(8,128)S(1)} fusion(f32[32,128]{1,0:T(8,128)S(1)} %convert_reduce_fusion, s32[256]{0:T(256)S(1)} %bitcast.85, f32[256,128]{1,0:T(8,128)S(1)} %bitcast.83), kind=kCustom, calls=%fused_computation.2 | custom fusion | flops 32768 | bytes 394240 | tf_op jit(solution)/shard_map/scatter-add | solution.py:47
  45.1 7.1 %fusion.29 = f32[32,128,512]{2,1,0:T(8,128)} fusion(bf16[32,128,512]{2,1,0:T(8,128)(2,1)} %bitcast.76, bf16[32,3,128,128]{3,2,1,0:T(8,128)(2,1)} %param.9), kind=kOutput, calls=%fused_computation.46 | convolution fusion | flops 536870912 | bytes 13631488 | tf_op jit(solution)/shard_map/itr,irc->itc/dot_general | solution.py:63
  52.2 5.7 %fusion.23 = f32[32,512,128]{1,2,0:T(8,128)} fusion(bf16[32,128,512]{2,1,0:T(8,128)(2,1)S(1)} %bitcast.77, bf16[1,128,512]{2,1,0:T(8,128)(2,1)S(1)} %collective-permute-done, bf16[32,3,128,128]{3,2,1,0:T(8,128)(2,1)} %param.9), kind=kOutput, calls=%fused_computation.40 | convolution fusion | flops 545259520 | bytes 13762560 | tf_op jit(solution)/shard_map/itr,irc->itc/dot_general | solution.py:63
  57.9 11.0 %all-to-all-done.1 = bf16[128,2,8,512]{3,2,1,0:T(8,128)(2,1)} async-done(((bf16[128,2,8,512]{3,2,1,0:T(8,128)(2,1)}), bf16[128,2,8,512]{3,2,1,0:T(8,128)(2,1)}, u32[]{:S(2)}, u32[]{:S(2)}) %all-to-all-start.1) | async-done | bytes 2097184 | tf_op jit(solution)/shard_map/all_to_all | solution.py:25
  68.9 12.9 %fusion.2 = f32[32,128,512]{2,1,0:T(8,128)} fusion(bf16[2048,512,1]{1,0,2:T(8,128)(2,1)} %bitcast.16, pred[32,2048]{1,0:T(8,128)(4,1)S(1)} %copy.25, bf16[2048,128]{0,1:T(8,128)(2,1)S(1)} %copy.26), kind=kOutput, calls=%fused_computation.5 | convolution fusion | flops 8598323200 | bytes 11075584 | tf_op jit(solution)/shard_map/tqr,qc->trc/dot_general | solution.py:66
  81.8 13.5 %multiply_reduce_fusion.1 = (f32[32,128]{1,0:T(8,128)S(1)}, f32[32,128,512]{2,1,0:T(8,128)}) fusion(f32[32,128]{1,0:T(8,128)S(1)} %scatter_fusion, f32[32,128,512]{2,1,0:T(8,128)} %fusion.2, bf16[1,128,512]{2,1,0:T(8,128)(2,1)S(1)} %collective-permute-done.1, bf16[32,128,512]{2,1,0:T(8,128)(2,1)S(1)} %bitcast.78, bf16[32,3,128,128]{3,2,1,0:T(8,128)(2,1)} %param.9, ...), kind=kOutput, calls=%fused_computation.24 | convolution fusion | flops 557838336 | bytes 38961152 | tf_op jit(solution)/shard_map/itr,irc->itc/dot_general | solution.py:63
  95.4 7.1 %fusion.8 = bf16[32,128,512]{2,1,0:T(8,128)(2,1)} fusion(f32[32,128,512]{2,1,0:T(8,128)} %get-tuple-element.9, f32[32,128]{1,0:T(8,128)S(1)} %maximum_multiply_fusion.1, pred[32,128]{1,0:T(8,128)(4,1)S(1)} %compare_bitcast_fusion, bf16[4096,512]{1,0:T(8,128)(2,1)S(1)} %copy-done.1), kind=kLoop, calls=%fused_computation.15 | loop fusion | flops 8388608 | bytes 16797696 | tf_op jit(solution)/shard_map/convert_element_type | solution.py:72
  102.5 4.3 %gather_fusion.1 = bf16[256,8,512]{2,1,0:T(8,128)(2,1)} fusion(bf16[512,8,512]{2,1,0:T(8,128)(2,1)} %bitcast.80, s32[1024]{0:T(1024)S(1)} %pad_clamp_fusion), kind=kCustom, calls=%fused_computation.1 | custom fusion | bytes 4195328 | tf_op jit(solution)/shard_map/gather | solution.py:24
  106.8 5.8 %all-to-all-start.2 = ((bf16[128,2,8,512]{3,2,1,0:T(8,128)(2,1)}), bf16[128,2,8,512]{3,2,1,0:T(8,128)(2,1)}, u32[]{:S(2)}, u32[]{:S(2)}) async-start(bf16[128,2,8,512]{3,2,1,0:T(8,128)(2,1)} %bitcast.82), calls=%async_computation.2 | async-start | bytes 4194304 | tf_op jit(solution)/shard_map/all_to_all | solution.py:25
  113.7 7.1 %fusion.27 = f32[32,512,128]{1,2,0:T(8,128)} fusion(bf16[32,128,512]{2,1,0:T(8,128)(2,1)} %fusion.8, bf16[32,3,128,128]{3,2,1,0:T(8,128)(2,1)} %param.9), kind=kOutput, calls=%fused_computation.44 | convolution fusion | flops 536870912 | bytes 13631488 | tf_op jit(solution)/shard_map/itr,irc->itc/dot_general | solution.py:63
  120.8 7.2 %collective-permute-start.3 = (bf16[1,128,512]{2,1,0:T(8,128)(2,1)S(1)}, bf16[1,128,512]{2,1,0:T(8,128)(2,1)S(1)}, u32[]{:S(2)}, u32[]{:S(2)}) collective-permute-start(bf16[1,128,512]{2,1,0:T(8,128)(2,1)S(1)} %get-tuple-element.4), channel_id=1, source_target_pairs={{1,0},{2,1},{3,2},{4,3},{5,4},{6,5},{7,6},{8,7},{9,8},{10,9},{11,1... | collective-permute-start | bytes 393224 | tf_op jit(solution)/shard_map/ppermute | solution.py:18
  127.9 15.6 %collective-permute-done.2 = bf16[1,128,512]{2,1,0:T(8,128)(2,1)S(1)} collective-permute-done((bf16[1,128,512]{2,1,0:T(8,128)(2,1)S(1)}, bf16[1,128,512]{2,1,0:T(8,128)(2,1)S(1)}, u32[]{:S(2)}, u32[]{:S(2)}) %collective-permute-start.2) | collective-permute-done | bytes 131104 | tf_op jit(solution)/shard_map/ppermute | solution.py:15
  143.6 5.7 %fusion.19 = f32[32,512,128]{1,2,0:T(8,128)} fusion(bf16[32,128,512]{2,1,0:T(8,128)(2,1)S(1)} %copy-done.3, bf16[1,128,512]{2,1,0:T(8,128)(2,1)S(1)} %collective-permute-done.2, bf16[32,3,128,128]{3,2,1,0:T(8,128)(2,1)} %param.9), kind=kOutput, calls=%fused_computation.34 | convolution fusion | flops 545259520 | bytes 13762560 | tf_op jit(solution)/shard_map/itr,irc->itc/dot_general | solution.py:63
  149.3 12.9 %fusion = f32[32,128,512]{2,1,0:T(8,128)} fusion(bf16[2048,512,1]{1,0,2:T(8,128)(2,1)} %bitcast.24, pred[32,2048]{1,0:T(8,128)(4,1)S(1)} %copy.25, bf16[2048,128]{0,1:T(8,128)(2,1)S(1)} %copy.26), kind=kOutput, calls=%fused_computation.3 | convolution fusion | flops 8598323200 | bytes 11075584 | tf_op jit(solution)/shard_map/tqr,qc->trc/dot_general | solution.py:66
  162.2 13.7 %multiply_reduce_fusion = (f32[32,128]{1,0:T(8,128)S(1)}, f32[32,128,512]{2,1,0:T(8,128)}) fusion(f32[32,128]{1,0:T(8,128)S(1)} %scatter_fusion, f32[32,128,512]{2,1,0:T(8,128)} %fusion, bf16[1,128,512]{2,1,0:T(8,128)(2,1)S(1)} %collective-permute-done.3, bf16[32,128,512]{2,1,0:T(8,128)(2,1)S(1)} %copy-done.4, bf16[32,3,128,128]{3,2,1,0:T(8,128)(2,1)} %param.9, ...), kind=kOutput, calls=%fused_computation.23 | convolution fusion | flops 557838336 | bytes 38961152 | tf_op jit(solution)/shard_map/itr,irc->itc/dot_general | solution.py:63
  175.9 5.0 %fusion.9 = bf16[32,128,512]{2,1,0:T(8,128)(2,1)S(1)} fusion(f32[32,128,512]{2,1,0:T(8,128)} %get-tuple-element.11, f32[32,128]{1,0:T(8,128)S(1)} %maximum_multiply_fusion, pred[32,128]{1,0:T(8,128)(4,1)S(1)} %compare_bitcast_fusion, bf16[4096,512]{1,0:T(8,128)(2,1)S(1)} %copy-done.2), kind=kLoop, calls=%fused_computation.16 | loop fusion | flops 8388608 | bytes 16797696 | tf_op jit(solution)/shard_map/convert_element_type | solution.py:72
  180.9 3.1 %fusion.11 = (f32[32]{0:T(128)S(1)}, f32[32]{0:T(128)S(1)}) fusion(bf16[32,128,512]{2,1,0:T(8,128)(2,1)S(1)} %bitcast.79, bf16[32,128,512]{2,1,0:T(8,128)(2,1)S(1)} %copy-done.4, bf16[32,128,512]{2,1,0:T(8,128)(2,1)S(1)} %fusion.9), kind=kLoop, calls=%fused_computation.18 | loop fusion | flops 18874304 | bytes 12583168 | tf_op jit(solution)/shard_map/reduce_sum | solution.py:74
  (45 shorter events, 6.3 us)
Async XLA Ops:
  2.0 22.8 %all-to-all-start = ((s32[1,128,2]{2,0,1:T(1,128)}), s32[1,128,2]{2,0,1:T(1,128)S(1)}, u32[]{:S(2)}, u32[]{:S(2)}) async-start(s32[1,128,2]{2,0,1:T(1,128)} %copy.27), calls=%async_computation | async-start | bytes 131072 | tf_op jit(solution)/shard_map/all_to_all | solution.py:40
  14.2 67.6 %collective-permute-start.1 = (bf16[1,128,512]{2,1,0:T(8,128)(2,1)S(1)}, bf16[1,128,512]{2,1,0:T(8,128)(2,1)S(1)}, u32[]{:S(2)}, u32[]{:S(2)}) collective-permute-start(bf16[1,128,512]{2,1,0:T(8,128)(2,1)S(1)} %get-tuple-element.6), channel_id=1, source_target_pairs={{1,0},{2,1},{3,2},{4,3},{5,4},{6,5},{7,6},{8,7},{9,8},{10,9},{11,1... | collective-permute-start | bytes 393224 | tf_op jit(solution)/shard_map/ppermute | solution.py:18
  21.3 30.9 %collective-permute-start = (bf16[1,128,512]{2,1,0:T(8,128)(2,1)S(1)}, bf16[1,128,512]{2,1,0:T(8,128)(2,1)S(1)}, u32[]{:S(2)}, u32[]{:S(2)}) collective-permute-start(bf16[1,128,512]{2,1,0:T(8,128)(2,1)S(1)} %get-tuple-element.7), channel_id=1, source_target_pairs={{0,1},{1,2},{2,3},{3,4},{4,5},{5,6},{6,7},{7,8},{8,9},{9,10},{10,1... | collective-permute-start | bytes 393224 | tf_op jit(solution)/shard_map/ppermute | solution.py:15
  25.0 14.8 %copy-start.6 = (bf16[1,128,2,8,128]{4,3,2,1,0:T(8,128)(2,1)S(1)}, bf16[1,128,2,8,128]{4,3,2,1,0:T(8,128)(2,1)}, u32[]{:S(2)}) copy-start(bf16[1,128,2,8,128]{4,3,2,1,0:T(8,128)(2,1)} %param.13) | copy-start | bytes 1572868
  29.4 39.5 %all-to-all-start.1 = ((bf16[128,2,8,512]{3,2,1,0:T(8,128)(2,1)}), bf16[128,2,8,512]{3,2,1,0:T(8,128)(2,1)}, u32[]{:S(2)}, u32[]{:S(2)}) async-start(bf16[128,2,8,512]{3,2,1,0:T(8,128)(2,1)} %bitcast.14), calls=%async_computation.1 | async-start | bytes 4194304 | tf_op jit(solution)/shard_map/all_to_all | solution.py:25
  45.0 7.2 %copy-start.7 = (s32[4096]{0:T(1024)S(1)}, s32[4096]{0:T(1024)}, u32[]{:S(2)}) copy-start(s32[4096]{0:T(1024)} %param.8) | copy-start | bytes 49156
  45.0 7.2 %copy-start = (bf16[4096,512]{1,0:T(8,128)(2,1)S(1)}, bf16[4096,512]{1,0:T(8,128)(2,1)}, u32[]{:S(2)}) copy-start(bf16[4096,512]{1,0:T(8,128)(2,1)} %param.7) | copy-start | bytes 12582916
  68.9 12.9 %copy-start.1 = (bf16[4096,512]{1,0:T(8,128)(2,1)S(1)}, bf16[4096,512]{1,0:T(8,128)(2,1)}, u32[]{:S(2)}) copy-start(bf16[4096,512]{1,0:T(8,128)(2,1)} %param.7) | copy-start | bytes 12582916
  106.8 42.5 %all-to-all-start.2 = ((bf16[128,2,8,512]{3,2,1,0:T(8,128)(2,1)}), bf16[128,2,8,512]{3,2,1,0:T(8,128)(2,1)}, u32[]{:S(2)}, u32[]{:S(2)}) async-start(bf16[128,2,8,512]{3,2,1,0:T(8,128)(2,1)} %bitcast.82), calls=%async_computation.2 | async-start | bytes 4194304 | tf_op jit(solution)/shard_map/all_to_all | solution.py:25
  113.6 30.0 %copy-start.3 = (bf16[32,128,512]{2,1,0:T(8,128)(2,1)S(1)}, bf16[32,128,512]{2,1,0:T(8,128)(2,1)}, u32[]{:S(2)}) copy-start(bf16[32,128,512]{2,1,0:T(8,128)(2,1)} %fusion.8) | copy-start | bytes 12582916
  113.6 30.0 %collective-permute-start.2 = (bf16[1,128,512]{2,1,0:T(8,128)(2,1)S(1)}, bf16[1,128,512]{2,1,0:T(8,128)(2,1)S(1)}, u32[]{:S(2)}, u32[]{:S(2)}) collective-permute-start(bf16[1,128,512]{2,1,0:T(8,128)(2,1)S(1)} %get-tuple-element.5), channel_id=1, source_target_pairs={{0,1},{1,2},{2,3},{3,4},{4,5},{5,6},{6,7},{7,8},{8,9},{9,10},{10,1... | collective-permute-start | bytes 393224 | tf_op jit(solution)/shard_map/ppermute | solution.py:15
  120.8 41.4 %collective-permute-start.3 = (bf16[1,128,512]{2,1,0:T(8,128)(2,1)S(1)}, bf16[1,128,512]{2,1,0:T(8,128)(2,1)S(1)}, u32[]{:S(2)}, u32[]{:S(2)}) collective-permute-start(bf16[1,128,512]{2,1,0:T(8,128)(2,1)S(1)} %get-tuple-element.4), channel_id=1, source_target_pairs={{1,0},{2,1},{3,2},{4,3},{5,4},{6,5},{7,6},{8,7},{9,8},{10,9},{11,1... | collective-permute-start | bytes 393224 | tf_op jit(solution)/shard_map/ppermute | solution.py:18
  149.3 12.9 %copy-start.4 = (bf16[32,128,512]{2,1,0:T(8,128)(2,1)S(1)}, bf16[32,128,512]{2,1,0:T(8,128)(2,1)}, u32[]{:S(2)}) copy-start(bf16[32,128,512]{2,1,0:T(8,128)(2,1)} %fusion.8) | copy-start | bytes 12582916
  162.2 13.7 %copy-start.2 = (bf16[4096,512]{1,0:T(8,128)(2,1)S(1)}, bf16[4096,512]{1,0:T(8,128)(2,1)}, u32[]{:S(2)}) copy-start(bf16[4096,512]{1,0:T(8,128)(2,1)} %param.7) | copy-start | bytes 12582916
  180.9 3.1 %copy-start.5 = (bf16[32,128,512]{2,1,0:T(8,128)(2,1)}, bf16[32,128,512]{2,1,0:T(8,128)(2,1)S(1)}, u32[]{:S(2)}) copy-start(bf16[32,128,512]{2,1,0:T(8,128)(2,1)S(1)} %fusion.9) | copy-start | bytes 12582916
where the time goes:
time: 185 us
  matrix products  78.7 us (43%)
  starting transfers between devices  40.9 us (22%)
  waiting for transfers between devices  26.7 us (14%)
  other arithmetic  23.1 us (12%)
  local copies, waits for them, and re-layouts  14.3 us (8%)
    dot_general x6, matrix products, body(): jnp.einsum('itr,irc->itc', band_w[:, offset + 1], source, preferred_eleme...  52.9 us
    dot_general x2, matrix products, body(): jnp.einsum('tqr,qc->trc', placed, received.reshape(-1, classes), preferre...  25.8 us
    ppermute x2, waiting for transfers between devices, with_halo(): lax.ppermute(lax.slice_in_dim(block, block.shape[dim] - width, None, axis...  15.6 us
    all_to_all x2, starting transfers between devices, fetch_blocks(): lax.all_to_all(blocks, 'node', split_axis=0, concat_axis=0, tiled=True)  15.4 us
    ppermute x2, starting transfers between devices, with_halo(): lax.ppermute(lax.slice_in_dim(block, 0, width, axis=dim), axis, backward)  14.3 us
    convert_element_type x2, other arithmetic, body(): fresh = jnp.where(seeded, clamped, scaled).astype(jnp.bfloat16)  12.1 us
    all_to_all x1, starting transfers between devices, body(): lax.all_to_all(far_block, 'node', split_axis=1, concat_axis=0, tiled=True)  11.2 us
    all_to_all x2, waiting for transfers between devices, fetch_blocks(): lax.all_to_all(blocks, 'node', split_axis=0, concat_axis=0, tiled=True)  11 us
  transfers between devices with their start and end apart: 7, of which 2 were waited for; matrix products, arithmetic and copies ran while one was open for 37% of the time, Pallas kernels for 0%

commit v1 on v0

v1 whole, which is shorter than its diff:
```python
import jax
import jax.numpy as jnp
from jax import lax
from jax.experimental import pallas as pl
from jax.experimental.pallas import tpu as pltpu
from jax.sharding import PartitionSpec as P

ITERS = 2
CAP = 16
GROUP = 4
F32 = jnp.float32
BF16 = jnp.bfloat16
VMEM = pl.BlockSpec(memory_space=pltpu.VMEM)
SMEM = pl.BlockSpec(memory_space=pltpu.SMEM)
ANY = pl.BlockSpec(memory_space=pltpu.HBM)
MIB = 1 << 20
DMA = pltpu.SemaphoreType.DMA


def in_hbm(x):
    return pltpu.with_memory_space_constraint(x, pltpu.HBM)


def in_vmem(x):
    return pltpu.with_memory_space_constraint(x, pltpu.VMEM)


def dot(a, b):
    return jnp.dot(a, b, preferred_element_type=F32)


def loop(low, high, step, unroll=1):
    def run(i, carry):
        step(i)
        return carry

    lax.fori_loop(low, high, run, 0, unroll=unroll)


def fold(row, width):
    total = row[:, :width]
    for j in range(1, row.shape[1] // width):
        total = total + row[:, j * width : (j + 1) * width]
    return total


def pick_kernel(got_ref, cur_ref, req_ref, send_ref, flat_ref, word_ref, held_ref, word_sem, in_sem, out_sem):
    slots, peers = req_ref.shape
    table = jnp.concatenate([got_ref[:, 0, :], jnp.zeros((peers, peers - slots), jnp.int32)], axis=1)
    flat_ref[...] = table.T[:8, :]
    move = pltpu.make_async_copy(flat_ref.at[pl.ds(0, slots)], word_ref, word_sem)
    move.start()
    move.wait()
    parts = in_sem.shape[0]
    share = peers // parts

    def fetch(d, part):
        for k in range(slots):
            row = word_ref[k, d]
            req_ref[k, d] = row
            pltpu.make_async_copy(cur_ref.at[row], held_ref.at[d * slots + k], in_sem.at[part]).start()

    for part in range(parts):
        loop(part * share, (part + 1) * share, lambda d: fetch(d, part), unroll=4)
    for part in range(parts):
        here = pl.ds(part * share * slots, share * slots)
        pltpu.make_async_copy(held_ref.at[here], held_ref.at[here], in_sem.at[part]).wait()
        pltpu.make_async_copy(held_ref.at[here], send_ref.at[here], out_sem.at[part]).start()
    for part in range(parts):
        here = pl.ds(part * share * slots, share * slots)
        pltpu.make_async_copy(held_ref.at[here], send_ref.at[here], out_sem.at[part]).wait()


def pick_blocks(got, blocks):
    peers, _, slots = got.shape
    shape = (peers * slots,) + blocks.shape[1:]
    return pl.pallas_call(
        pick_kernel,
        out_shape=(jax.ShapeDtypeStruct((slots, peers), jnp.int32), pltpu.HBM(shape, BF16)),
        in_specs=[VMEM, ANY],
        out_specs=(SMEM, ANY),
        scratch_shapes=[
            pltpu.VMEM((8, peers), jnp.int32),
            pltpu.SMEM((slots, peers), jnp.int32),
            pltpu.VMEM(shape, BF16),
            DMA,
            DMA((4,)),
            DMA((4,)),
        ],
        cost_estimate=pl.CostEstimate(flops=1_000_000_000, bytes_accessed=4_000_000, transcendentals=0),
        compiler_params=pltpu.CompilerParams(vmem_limit_bytes=32 * MIB),
        name="pick",
    )(in_vmem(got), in_hbm(blocks))


def band_sum(band_ref, cur_ref, t, tiles, rows):
    def rows_of(first, n):
        return cur_ref[pl.ds(pl.multiple_of(first * rows, rows), n * rows), :]

    def join(offsets):
        return jnp.concatenate([band_ref[t, o] for o in offsets], axis=1)

    if isinstance(t, int) and t == 0:
        return dot(join((1, 2)), rows_of(0, 2))
    if isinstance(t, int) and t == tiles - 1:
        return dot(join((0, 1)), rows_of(tiles - 2, 2))
    return dot(join((0, 1, 2)), rows_of(t - 1, 3))


def prep_kernel(
    tile_ref, count_ref, seed_ref, far_ref, band_hbm, lab_hbm,
    table_ref, mat_hbm, aux_ref, edge_ref, base_hbm,
    cnt_ref, num_ref, band_ref, lab_ref, out_ref, deg_ref, mat_ref, in_sem, out_sem, mat_sem,
):
    peers = count_ref.shape[0]
    total = tile_ref.shape[0]
    slots = total // peers
    tiles, _, rows, _ = band_ref.shape
    chunks = mat_ref.shape[0]
    num_at, ext_at, used_at = chunks * CAP, chunks * CAP + tiles, chunks * CAP + chunks
    get_band = pltpu.make_async_copy(band_hbm, band_ref, in_sem.at[0])
    get_lab = pltpu.make_async_copy(lab_hbm, lab_ref, in_sem.at[1])
    get_band.start()
    get_lab.start()

    def clear(i):
        table_ref[i] = 0

    loop(0, table_ref.shape[0], clear, unroll=16)

    def clear_count(i):
        cnt_ref[i] = 0
        num_ref[i] = 0

    loop(0, chunks, clear_count, unroll=8)

    def scan(peer):
        live = count_ref[peer]
        for k in range(slots):
            @pl.when(k < live)
            def _():
                tile = tile_ref[k * peers + peer]
                place = num_ref[tile]
                num_ref[tile] = place + 1
                slot = peer * slots + k

                @pl.when(place < CAP)
                def _():
                    table_ref[tile * CAP + place] = slot

                @pl.when(place >= CAP)
                def _():
                    inner = lax.rem(place, CAP)

                    @pl.when(inner == 0)
                    def _():
                        fresh = table_ref[used_at]
                        table_ref[ext_at + fresh] = tile
                        table_ref[used_at] = fresh + 1

                    def find(c, last):
                        return jnp.where(table_ref[ext_at + c] == tile, c, last)

                    chunk = tiles + lax.fori_loop(0, table_ref[used_at], find, 0)
                    table_ref[chunk * CAP + inner] = slot
                    cnt_ref[chunk] = inner + 1

    loop(0, peers, scan, unroll=2)

    def tidy(t):
        cnt_ref[t] = jnp.minimum(num_ref[t], CAP)
        table_ref[num_at + t] = num_ref[t]

    loop(0, tiles, tidy)

    def seeded(t):
        return jnp.broadcast_to(seed_ref[t].astype(F32), (rows, rows)).T == 1.0

    def build(c, free):
        parts = [far_ref[table_ref[c * CAP + p]].astype(F32) for p in range(CAP)]
        mat = jnp.concatenate(parts, axis=0)
        depth = lax.broadcasted_iota(jnp.int32, mat.shape, 0)
        mat = jnp.where(depth < cnt_ref[c] * far_ref.shape[1], mat, 0.0).T
        mat_ref[c] = jnp.where(free, mat, 0.0).astype(BF16)
        return mat

    get_band.wait()
    get_lab.wait()

    def copy_of(t):
        return pltpu.make_async_copy(out_ref.at[t], base_hbm.at[t], out_sem.at[t])

    def tile_step(t):
        seed = seeded(t)
        free = jnp.logical_not(seed)
        w = band_ref[t].astype(F32)
        degree = jnp.sum(w[0] + w[1] + w[2] + build(t, free), axis=1, keepdims=True)
        deg_ref[t] = jnp.broadcast_to(degree, (rows, rows))
        here = lab_ref[pl.ds(pl.multiple_of(t * rows, rows), rows), :].astype(F32)
        out_ref[t] = jnp.where(seed[:, :1], here, band_sum(band_ref, lab_ref, t, tiles, rows))
        copy_of(t).start()

    tile_step(0)
    loop(1, tiles - 1, tile_step)
    tile_step(tiles - 1)

    def extra_step(c):
        t = table_ref[ext_at + c]
        mat = build(tiles + c, jnp.logical_not(seeded(t)))
        deg_ref[t] = deg_ref[t] + jnp.sum(mat, axis=1, keepdims=True)

    loop(0, table_ref[used_at], extra_step)
    put_mat = pltpu.make_async_copy(mat_ref, mat_hbm, mat_sem)
    put_mat.start()
    lane = lax.broadcasted_iota(jnp.int32, (rows, rows), 1)
    aux_ref[...] = jnp.ones_like(aux_ref)

    def finish(t):
        inv = 1.0 / deg_ref[t]
        aux_ref[...] = jnp.where(lane == t, jnp.where(seeded(t), -inv, inv), aux_ref[...])

    loop(0, tiles, finish)
    for side, (t, o) in enumerate(((0, 0), (tiles - 1, 2))):
        edge_ref[side] = jnp.where(seeded(t), 0.0, band_ref[t, o].astype(F32)).astype(BF16)
    loop(0, tiles, lambda t: copy_of(t).wait())
    put_mat.wait()


def prepare(far_tile, far_count, far_w, band_w, seed_rows, labels):
    tiles, _, rows, _ = band_w.shape
    classes = labels.shape[1]
    total = far_tile.shape[0]
    chunks = tiles + total // CAP
    table = -(-(chunks * CAP + chunks + 1) // 128) * 128
    return pl.pallas_call(
        prep_kernel,
        out_shape=(
            jax.ShapeDtypeStruct((table,), jnp.int32),
            pltpu.HBM((chunks, rows, CAP * far_w.shape[1]), BF16),
            jax.ShapeDtypeStruct((rows, rows), F32),
            jax.ShapeDtypeStruct((2, rows, rows), BF16),
            pltpu.HBM((tiles, rows, classes), F32),
        ),
        in_specs=[SMEM, SMEM, VMEM, VMEM, ANY, ANY],
        out_specs=(SMEM, ANY, VMEM, VMEM, ANY),
        scratch_shapes=[
            pltpu.SMEM((chunks,), jnp.int32),
            pltpu.SMEM((chunks,), jnp.int32),
            pltpu.VMEM(band_w.shape, BF16),
            pltpu.VMEM(labels.shape, BF16),
            pltpu.VMEM((tiles, rows, classes), F32),
            pltpu.VMEM((tiles, rows, rows), F32),
            pltpu.VMEM((chunks, rows, CAP * far_w.shape[1]), BF16),
            DMA((2,)),
            DMA((tiles,)),
            DMA,
        ],
        cost_estimate=pl.CostEstimate(flops=10_000_000_000, bytes_accessed=16_000_000, transcendentals=0),
        compiler_params=pltpu.CompilerParams(vmem_limit_bytes=32 * MIB),
        name="prep",
    )(far_tile, far_count, seed_rows, far_w, in_hbm(band_w), in_hbm(labels))


def band_kernel(aux_ref, band_hbm, cur_hbm, old_hbm, base_hbm, res_ref, band_ref, cur_ref, old_ref, out_ref, part_ref, in_sem, out_sem):
    tiles, _, rows, _ = band_ref.shape
    gets = [
        pltpu.make_async_copy(src, dst, in_sem.at[i])
        for i, (src, dst) in enumerate(((band_hbm, band_ref), (cur_hbm, cur_ref), (old_hbm, old_ref)))
    ]
    for get in gets:
        get.start()
    part_ref[...] = jnp.zeros_like(part_ref)
    lane = lax.broadcasted_iota(jnp.int32, (rows, rows), 1)
    for get in gets:
        get.wait()

    def copy_of(t):
        return pltpu.make_async_copy(out_ref.at[t], base_hbm.at[t], out_sem.at[t])

    def step(t):
        place = pl.ds(pl.multiple_of(t * rows, rows), rows)
        here = cur_ref[place, :].astype(F32)
        seed = jnp.sum(jnp.where(lane == t, aux_ref[...], 0.0), axis=1, keepdims=True) < 0.0
        out_ref[t] = jnp.where(seed, here, band_sum(band_ref, cur_ref, t, tiles, rows))
        copy_of(t).start()
        gap = jnp.abs(here - old_ref[place, :].astype(F32))
        part_ref[pl.ds(t, 1), :] = fold(jnp.sum(gap, axis=0, keepdims=True), rows)

    step(0)
    loop(1, tiles - 1, step)
    step(tiles - 1)
    res_ref[...] = jnp.sum(part_ref[...].T, axis=0, keepdims=True)
    loop(0, tiles, lambda t: copy_of(t).wait())


def band_sums(aux, band_w, current, old):
    tiles, _, rows, _ = band_w.shape
    classes = current.shape[1]
    return pl.pallas_call(
        band_kernel,
        out_shape=(pltpu.HBM((tiles, rows, classes), F32), jax.ShapeDtypeStruct((1, rows), F32)),
        in_specs=[VMEM, ANY, ANY, ANY],
        out_specs=(ANY, VMEM),
        scratch_shapes=[
            pltpu.VMEM(band_w.shape, BF16),
            pltpu.VMEM(current.shape, BF16),
            pltpu.VMEM(current.shape, BF16),
            pltpu.VMEM((tiles, rows, classes), F32),
            pltpu.VMEM((rows, rows), F32),
            DMA((3,)),
            DMA((tiles,)),
        ],
        cost_estimate=pl.CostEstimate(flops=10_000_000_000, bytes_accessed=16_000_000, transcendentals=0),
        compiler_params=pltpu.CompilerParams(vmem_limit_bytes=32 * MIB),
        name="band",
    )(aux, in_hbm(band_w), in_hbm(current), in_hbm(old))


def far_kernel(first, *refs):
    if first:
        (table_ref, req_ref, aux_ref, low_ref, high_ref, edge_ref, recv_ref, mat_hbm, base_hbm,
         new_hbm, send_hbm, top_ref, end_ref,
         mat_ref, base_ref, new_ref, in_sem, rest_sem, out_sem, send_ref, send_sem) = refs
    else:
        (table_ref, res_ref, aux_ref, low_ref, high_ref, edge_ref, recv_ref, mat_hbm, base_hbm, cur_hbm,
         new_hbm, both_ref,
         mat_ref, base_ref, new_ref, in_sem, rest_sem, out_sem, cur_ref, part_ref) = refs
    tiles, rows, classes = base_ref.shape
    chunks = mat_ref.shape[0]
    num_at, ext_at, used_at = chunks * CAP, chunks * CAP + tiles, chunks * CAP + chunks
    block = new_ref.shape[1]
    per = rows // block

    def group_copies(g):
        here = pl.ds(g * GROUP, GROUP)
        copies = [
            pltpu.make_async_copy(mat_hbm.at[here], mat_ref.at[here], in_sem.at[0, g]),
            pltpu.make_async_copy(base_hbm.at[here], base_ref.at[here], in_sem.at[1, g]),
        ]
        if not first:
            wide = pl.ds(g * GROUP * per, GROUP * per)
            copies.append(pltpu.make_async_copy(cur_hbm.at[wide], cur_ref.at[wide], in_sem.at[2, g]))
        return copies

    groups = tiles // GROUP
    for g in range(groups):
        for copy in group_copies(g):
            copy.start()
    rest = pl.ds(tiles, chunks - tiles)
    get_rest = pltpu.make_async_copy(mat_hbm.at[rest], mat_ref.at[rest], rest_sem)

    @pl.when(table_ref[used_at] > 0)
    def _():
        get_rest.start()
        get_rest.wait()

    if not first:
        part_ref[...] = jnp.zeros_like(part_ref)
    lane = lax.broadcasted_iota(jnp.int32, (rows, rows), 1)

    def gathered(c):
        parts = [recv_ref[table_ref[c * CAP + p]].astype(F32) for p in range(CAP)]
        return jnp.concatenate(parts, axis=0).astype(BF16)

    def out_copy(t):
        here = pl.ds(t * per, per)
        return pltpu.make_async_copy(new_ref.at[here], new_hbm.at[here], out_sem.at[t])

    def use(t, acc):
        here = pl.ds(t * per, per)
        signed = jnp.sum(jnp.where(lane == t, aux_ref[...], 0.0), axis=1, keepdims=True)
        mean = jnp.sum(acc * acc, axis=1, keepdims=True) * (1.0 / classes)
        scale = jnp.where(signed < 0.0, 1.0, signed / jnp.maximum(signed * jnp.sqrt(mean), 0.05))
        fresh = (acc * scale).astype(BF16)
        new_ref[here] = fresh.astype(F32).reshape(per, block, classes).astype(BF16)
        if not first:
            gap = jnp.abs(fresh.astype(F32) - cur_ref[here].astype(F32).reshape(rows, classes))
            part_ref[pl.ds(t, 1), :] = fold(jnp.sum(gap, axis=0, keepdims=True), rows)

    def tile_step(t):
        use(t, base_ref[t] + dot(mat_ref[t], gathered(t)))
        out_copy(t).start()

    def group_step(g):
        for copy in group_copies(g):
            copy.wait()

        @pl.when(g == 0)
        def _():
            base_ref[0] += dot(edge_ref[0], low_ref[...])

        @pl.when(g == groups - 1)
        def _():
            base_ref[tiles - 1] += dot(edge_ref[1], high_ref[...])

        def extra(c):
            t = table_ref[ext_at + c]

            @pl.when(lax.div(t, GROUP) == g)
            def _():
                base_ref[t] += dot(mat_ref[tiles + c], gathered(tiles + c))

        loop(0, table_ref[used_at], extra)
        for i in range(GROUP):
            tile_step(g * GROUP + i)

    loop(0, groups, group_step)
    if first:
        peers = req_ref.shape[1]
        parts = send_sem.shape[0]
        share = peers // parts

        def send_copy(part):
            here = pl.ds(part * share * req_ref.shape[0], share * req_ref.shape[0])
            return pltpu.make_async_copy(send_ref.at[here], send_hbm.at[here], send_sem.at[part])

        def choose(d):
            for k in range(req_ref.shape[0]):
                send_ref[d * req_ref.shape[0] + k] = new_ref[req_ref[k, d]]

        for part in range(parts):
            loop(part * share, (part + 1) * share, choose, unroll=8)
            send_copy(part).start()
        top_ref[...] = new_ref[0:per]
        end_ref[...] = new_ref[(tiles - 1) * per :]
        for part in range(parts):
            send_copy(part).wait()
    else:
        last = jnp.sum(part_ref[...].T, axis=0, keepdims=True)
        both_ref[0:1, :] = res_ref[:, :tiles]
        both_ref[1:2, :] = last[:, :tiles]
    loop(0, tiles, lambda t: out_copy(t).wait())


def far_call(first, args, tiles, rows, classes, chunks, total, block):
    blocks = pltpu.HBM((tiles * rows // block, block, classes), BF16)
    half = jax.ShapeDtypeStruct((rows // block, block, classes), BF16)
    picked = pltpu.HBM((total, block, classes), BF16)
    scratch = [
        pltpu.VMEM((chunks, rows, CAP * block), BF16),
        pltpu.VMEM((tiles, rows, classes), F32),
        pltpu.VMEM(blocks.shape, BF16),
        DMA((3, tiles // GROUP)),
        DMA,
        DMA((tiles,)),
    ]
    if first:
        outs, specs = (blocks, picked, half, half), (ANY, ANY, VMEM, VMEM)
        ins = [SMEM, SMEM] + [VMEM] * 5 + [ANY] * 2
        scratch += [pltpu.VMEM(picked.shape, BF16), DMA((4,))]
    else:
        outs, specs = (blocks, jax.ShapeDtypeStruct((ITERS, tiles), F32)), (ANY, VMEM)
        ins = [SMEM] + [VMEM] * 6 + [ANY] * 3
        scratch += [pltpu.VMEM(blocks.shape, BF16), pltpu.VMEM((rows, rows), F32)]
    return pl.pallas_call(
        lambda *refs: far_kernel(first, *refs),
        out_shape=outs,
        in_specs=ins,
        out_specs=specs,
        scratch_shapes=scratch,
        cost_estimate=pl.CostEstimate(flops=4_000_000_000, bytes_accessed=18_000_000, transcendentals=0),
        compiler_params=pltpu.CompilerParams(vmem_limit_bytes=32 * MIB),
        name="far_first" if first else "far_last",
    )(*args)


def halos(first, last):
    count = lax.axis_size("node")
    forward = [(i, (i + 1) % count) for i in range(count)]
    backward = [(target, source) for source, target in forward]
    return lax.ppermute(last, "node", forward), lax.ppermute(first, "node", backward)


def body(labels, seed_mask, band_w, far_block, far_tile, far_count, far_w):
    node_rows, classes = labels.shape
    tiles, _, rows, _ = band_w.shape
    _, peers, slots, block, _ = far_w.shape
    total = peers * slots
    got = lax.all_to_all(far_block, "node", split_axis=1, concat_axis=0, tiled=True)
    blocks = labels.reshape(-1, block, classes)
    requests, send = pick_blocks(got, blocks)

    def exchange(x):
        x = x.reshape(peers, slots, block, classes)
        return lax.all_to_all(x, "node", split_axis=0, concat_axis=0, tiled=True).reshape(total, block, classes)

    recv = exchange(send)
    low, high = halos(labels[:rows], labels[-rows:])
    table, mat, aux, edges, base = prepare(
        far_tile[0].T.reshape(total), far_count[0], far_w.reshape(total, block, rows), band_w,
        seed_mask.reshape(tiles, 1, rows), labels,
    )
    sizes = (tiles, rows, classes, mat.shape[0], total, block)
    new, send, top, end = far_call(True, (table, requests, aux, low, high, edges, in_vmem(recv), in_hbm(mat), in_hbm(base)), *sizes)
    recv = exchange(send)
    low, high = halos(top.reshape(rows, classes), end.reshape(rows, classes))
    base, change = band_sums(aux, band_w, new.reshape(node_rows, classes), labels)
    final, both = far_call(False, (table, change, aux, low, high, edges, in_vmem(recv), in_hbm(mat), in_hbm(base), in_hbm(new)), *sizes)
    return final.reshape(node_rows, classes), both


def solution(mesh):
    placed = (
        P("node", None),
        P("node"),
        P("node", None, None, None),
        P("node", None, None),
        P("node", None, None),
        P("node", None),
        P("node", None, None, None, None),
    )
    return jax.shard_map(
        body,
        mesh=mesh,
        in_specs=placed,
        out_specs=(P("node", None), P(None, "node")),
        check_vma=False,
    )
```

time: 185 us -> 119 us (0.64)
  matrix products: 78.7 us -> 0 us
  Pallas kernels: 0 us -> 56.5 us
  other arithmetic: 23.1 us -> 0 us
  blocking collectives: 0 us -> 20.3 us
  starting transfers between devices: 40.9 us -> 25.8 us
  waiting for transfers between devices: 26.7 us -> 13.8 us
  local copies, waits for them, and re-layouts: 14.3 us -> 1.79 us
    dot_general x8 -> x0, matrix products: 78.7 us -> none  [the longest x6 52.9 us: body(): jnp.einsum('itr,irc->itc', band_w[:, offset + 1], source, preferred_eleme...]
    pallas_call x0 -> x5, Pallas kernels: none -> 56.5 us  [the longest x1 21.2 us: prepare(): pl.pallas_call(prep_kernel, out_shape=(jax.ShapeDtypeStruct((table,), jnp...]
    all_to_all x0 -> x1, blocking collectives: none -> 20.3 us  [body(): lax.all_to_all(far_block, 'node', split_axis=1, concat_axis=0, tiled=True)]
    all_to_all x3 -> x2, starting transfers between devices: 26.6 us -> 11.6 us  [exchange(): lax.all_to_all(x, 'node', split_axis=0, concat_axis=0, tiled=True)]
    convert_element_type x2 -> x0, other arithmetic: 12.1 us -> none  [body(): fresh = jnp.where(seeded, clamped, scaled).astype(jnp.bfloat16)]
    all_to_all x3 -> x2, waiting for transfers between devices: 11 us -> 0.01 us  [exchange(): lax.all_to_all(x, 'node', split_axis=0, concat_axis=0, tiled=True)]
    gather x2 -> x0, local copies, waits for them, and re-layouts: 8.59 us -> none  [fetch_blocks(): blocks = current.reshape(-1, block_rows, classes)[requests]]
    reduce_sum x3 -> x0, other arithmetic: 6.08 us -> none  [the longest x1 3.05 us: body(): jnp.sum(jnp.abs(fresh.astype(jnp.float32) - previous), axis=(1, 2))]
  transfers between devices with their start and end apart: 7 -> 6, of which waited for: 2 -> 3; matrix products, arithmetic and copies ran while one was open for 37% -> 1% of each run, Pallas kernels for 0% -> 29%
where the time goes in v1:
time: 119 us
  Pallas kernels  56.5 us (47%)
  starting transfers between devices  25.8 us (22%)
  blocking collectives  20.3 us (17%)
  waiting for transfers between devices  13.8 us (12%)
  local copies, waits for them, and re-layouts  1.79 us (2%)
    pallas_call x1, Pallas kernels, prepare(): pl.pallas_call(prep_kernel, out_shape=(jax.ShapeDtypeStruct((table,), jnp...  21.2 us
    all_to_all x1, blocking collectives, body(): lax.all_to_all(far_block, 'node', split_axis=1, concat_axis=0, tiled=True)  20.3 us
    pallas_call x2, Pallas kernels, far_call(): pl.pallas_call(lambda *refs: far_kernel(first, *refs), out_shape=outs, in...  18.4 us
    ppermute x2, starting transfers between devices, halos(): lax.ppermute(first, 'node', backward)  14.2 us
    pallas_call x1, Pallas kernels, band_sums(): pl.pallas_call(band_kernel, out_shape=(pltpu.HBM((tiles, rows, classes),...  12.8 us
    all_to_all x2, starting transfers between devices, exchange(): lax.all_to_all(x, 'node', split_axis=0, concat_axis=0, tiled=True)  11.6 us
    ppermute x2, waiting for transfers between devices, halos(): lax.ppermute(last, 'node', forward)  10.6 us
    pallas_call x1, Pallas kernels, pick_blocks(): pl.pallas_call(pick_kernel, out_shape=(jax.ShapeDtypeStruct((slots, peers...  4.05 us
  transfers between devices with their start and end apart: 6, of which 3 were waited for; matrix products, arithmetic and copies ran while one was open for 1% of the time, Pallas kernels for 29%

profile of v1, /device:TPU:0, one launch (start us, length us, event | category | flops | bytes accessed | tf_op | source)
XLA Modules:
  0.0 118.9 jit_solution(8393717985333259089)
XLA Ops:
  0.6 0.8 copy.10
  1.4 20.3 %all_to_all.22 = s32[1,128,2]{2,0,1:T(1,128)S(1)} all-to-all(s32[1,128,2]{2,0,1:T(1,128)S(1)} %copy.10), channel_id=1, replica_groups=mesh['node'=128] {'node'}, dimensions={1} | all-to-all | bytes 2048 | tf_op jit(solution)/shard_map/all_to_all | solution.py:479
  21.7 4.1 %pick.1 = (s32[2,128]{1,0:T(2,128)S(1)}, bf16[256,8,512]{2,1,0:T(8,128)(2,1)}) custom-call(s32[128,1,2]{2,1,0:T(1,128)S(1)} %bitcast.20, bf16[512,8,512]{2,1,0:T(8,128)(2,1)} %bitcast.27), custom_call_target="tpu_custom_call" | custom-call | flops 1000000000 | bytes 4000000 | tf_op jit(solution)/shard_map/pick/pallas_call | solution.py:77
  25.8 4.7 %all-to-all-start.1 = ((bf16[128,2,8,512]{3,2,1,0:T(8,128)(2,1)}), bf16[128,2,8,512]{3,2,1,0:T(8,128)(2,1)S(1)}, u32[]{:S(2)}, u32[]{:S(2)}) async-start(bf16[128,2,8,512]{3,2,1,0:T(8,128)(2,1)} %bitcast.29), calls=%async_computation.1 | async-start | bytes 4194304 | tf_op jit(solution)/shard_map/all_to_all | solution.py:485
  30.5 1.0 fusion
  31.5 7.1 %collective-permute-start.1 = (bf16[128,512]{1,0:T(8,128)(2,1)S(1)}, bf16[128,512]{1,0:T(8,128)(2,1)S(1)}, u32[]{:S(2)}, u32[]{:S(2)}) collective-permute-start(bf16[128,512]{1,0:T(8,128)(2,1)S(1)} %get-tuple-element.32), channel_id=1, source_target_pairs={{1,0},{2,1},{3,2},{4,3},{5,4},{6,5},{7,6},{8,7},{9,8},{10,9},{11,1... | collective-permute-start | bytes 393224 | tf_op jit(solution)/shard_map/ppermute | solution.py:471
  38.6 0.0 collective-permute-start
  38.6 0.0 copy-done
  38.6 0.0 copy-done.1
  38.6 0.0 copy-done.2
  38.6 0.0 copy-done.3
  38.6 21.2 %prep.1 = (s32[896]{0:T(1024)S(1)}, bf16[48,128,128]{2,1,0:T(8,128)(2,1)}, f32[128,128]{1,0:T(8,128)S(1)}, bf16[2,128,128]{2,1,0:T(8,128)(2,1)S(1)}, f32[32,128,512]{2,1,0:T(8,128)}) custom-call(s32[256]{0:T(256)S(1)} %bitcast.25, s32[128]{0:T(128)S(1)} %bitcast.26, s32[32,1,128]{2,1,0:T(1,128)S(1)} %bitcast.24, bf16[256,8,128]{2,1,0:T(8,128)(2,1)S(1)} %bitcast.21, ...), custom_call_target="tpu_custom_call" | custom-call | flops 10000000000 | bytes 16000000 | tf_op jit(solution)/shard_map/prep/pallas_call | solution.py:235
  59.9 0.0 collective-permute-done.1.refs_4_
  59.9 2.2 %collective-permute-done.refs_3_ = bf16[128,512]{1,0:T(8,128)(2,1)S(1)} collective-permute-done((bf16[128,512]{1,0:T(8,128)(2,1)S(1)}, bf16[128,512]{1,0:T(8,128)(2,1)S(1)}, u32[]{:S(2)}, u32[]{:S(2)}) %collective-permute-start) | collective-permute-done | bytes 131104 | tf_op jit(solution)/shard_map/ppermute | solution.py:471
  62.0 0.0 all-to-all-done.1
  62.0 8.4 %far_first.1 = (bf16[512,8,512]{2,1,0:T(8,128)(2,1)}, bf16[256,8,512]{2,1,0:T(8,128)(2,1)}, bf16[16,8,512]{2,1,0:T(8,128)(2,1)S(1)}, bf16[16,8,512]{2,1,0:T(8,128)(2,1)S(1)}) custom-call(s32[896]{0:T(1024)S(1)} %get-tuple-element.17.refs_0_, s32[2,128]{1,0:T(2,128)S(1)} %get-tuple-element.19.refs_1_, f32[128,128]{1,0:T(8,128)S(1)} %get-tuple-element.18.refs_2_.aux_ref, ...), custom_call_target="tpu_custom_call" | custom-call | flops 4000000000 | bytes 18000000 | tf_op jit(solution)/shard_map/far_first/pallas_call | solution.py:455
  70.4 6.9 %all-to-all-start.2 = ((bf16[128,2,8,512]{3,2,1,0:T(8,128)(2,1)}), bf16[128,2,8,512]{3,2,1,0:T(8,128)(2,1)S(1)}, u32[]{:S(2)}, u32[]{:S(2)}) async-start(bf16[128,2,8,512]{3,2,1,0:T(8,128)(2,1)} %bitcast.30), calls=%async_computation.2 | async-start | bytes 4194304 | tf_op jit(solution)/shard_map/all_to_all | solution.py:485
  77.3 7.1 %collective-permute-start.3 = (bf16[128,512]{1,0:T(8,128)(2,1)S(1)}, bf16[128,512]{1,0:T(8,128)(2,1)S(1)}, u32[]{:S(2)}, u32[]{:S(2)}) collective-permute-start(bf16[128,512]{1,0:T(8,128)(2,1)S(1)} %bitcast.23), channel_id=1, source_target_pairs={{1,0},{2,1},{3,2},{4,3},{5,4},{6,5},{7,6},{8,7},{9,8},{10,9},{11,1... | collective-permute-start | bytes 393224 | tf_op jit(solution)/shard_map/ppermute | solution.py:471
  84.4 0.0 collective-permute-start.2
  84.4 12.8 %band.1 = (f32[32,128,512]{2,1,0:T(8,128)}, f32[1,128]{1,0:T(1,128)S(1)}) custom-call(f32[128,128]{1,0:T(8,128)S(1)} %get-tuple-element.18.refs_2_.aux_ref, bf16[32,3,128,128]{3,2,1,0:T(8,128)(2,1)} %band_hbm.3, bf16[4096,512]{1,0:T(8,128)(2,1)} %bitcast.28, bf16[4096,512]{1,0:T(8,128)(2,1)} %old_hbm.1), custom_call_target="tpu_custom_call" | custom-call | flops 10000000000 | bytes 16000000 | tf_op jit(solution)/shard_map/band/pallas_call | solution.py:299
  97.2 3.2 %collective-permute-done.3.refs_4_ = bf16[128,512]{1,0:T(8,128)(2,1)S(1)} collective-permute-done((bf16[128,512]{1,0:T(8,128)(2,1)S(1)}, bf16[128,512]{1,0:T(8,128)(2,1)S(1)}, u32[]{:S(2)}, u32[]{:S(2)}) %collective-permute-start.3) | collective-permute-done | bytes 131104 | tf_op jit(solution)/shard_map/ppermute | solution.py:471
  100.4 8.5 %collective-permute-done.2.refs_3_ = bf16[128,512]{1,0:T(8,128)(2,1)S(1)} collective-permute-done((bf16[128,512]{1,0:T(8,128)(2,1)S(1)}, bf16[128,512]{1,0:T(8,128)(2,1)S(1)}, u32[]{:S(2)}, u32[]{:S(2)}) %collective-permute-start.2) | collective-permute-done | bytes 131104 | tf_op jit(solution)/shard_map/ppermute | solution.py:471
  108.9 0.0 all-to-all-done.2
  108.9 10.0 %far_last.1 = (bf16[512,8,512]{2,1,0:T(8,128)(2,1)}, f32[2,32]{1,0:T(2,128)}) custom-call(s32[896]{0:T(1024)S(1)} %get-tuple-element.17.refs_0_, f32[1,128]{1,0:T(1,128)S(1)} %get-tuple-element.25.refs_1_, f32[128,128]{1,0:T(8,128)S(1)} %get-tuple-element.18.refs_2_.aux_ref, bf16[128,512]{1,0:T(8,128)(2,1)S(1)} %collective-permute-done.2.refs_3_, ...), custom_call_target="tpu_custom_call" | custom-call | flops 4000000000 | bytes 18000000 | tf_op jit(solution)/shard_map/far_last/pallas_call | solution.py:455
  (4 shorter events, 0.0 us)
Async XLA Ops:
  21.7 16.8 %copy-start = (bf16[1,128,2,8,128]{4,3,2,1,0:T(8,128)(2,1)S(1)}, bf16[1,128,2,8,128]{4,3,2,1,0:T(8,128)(2,1)}, u32[]{:S(2)}) copy-start(bf16[1,128,2,8,128]{4,3,2,1,0:T(8,128)(2,1)} %param.13) | copy-start | bytes 1572868
  21.7 16.8 %copy-start.1 = (s32[4096]{0:T(1024)S(1)}, s32[4096]{0:T(1024)}, u32[]{:S(2)}) copy-start(s32[4096]{0:T(1024)} %param.8) | copy-start | bytes 49156
  21.7 16.9 %copy-start.2 = (s32[1,128,2]{1,2,0:T(2,128)S(1)}, s32[1,128,2]{1,2,0:T(2,128)}, u32[]{:S(2)}) copy-start(s32[1,128,2]{1,2,0:T(2,128)} %param.11) | copy-start | bytes 3076
  21.7 16.9 %copy-start.3 = (s32[1,128]{1,0:T(1,128)S(1)}, s32[1,128]{1,0:T(1,128)}, u32[]{:S(2)}) copy-start(s32[1,128]{1,0:T(1,128)} %param.12) | copy-start | bytes 1540
  25.8 36.2 %all-to-all-start.1 = ((bf16[128,2,8,512]{3,2,1,0:T(8,128)(2,1)}), bf16[128,2,8,512]{3,2,1,0:T(8,128)(2,1)S(1)}, u32[]{:S(2)}, u32[]{:S(2)}) async-start(bf16[128,2,8,512]{3,2,1,0:T(8,128)(2,1)} %bitcast.29), calls=%async_computation.1 | async-start | bytes 4194304 | tf_op jit(solution)/shard_map/all_to_all | solution.py:485
  31.5 28.4 %collective-permute-start.1 = (bf16[128,512]{1,0:T(8,128)(2,1)S(1)}, bf16[128,512]{1,0:T(8,128)(2,1)S(1)}, u32[]{:S(2)}, u32[]{:S(2)}) collective-permute-start(bf16[128,512]{1,0:T(8,128)(2,1)S(1)} %get-tuple-element.32), channel_id=1, source_target_pairs={{1,0},{2,1},{3,2},{4,3},{5,4},{6,5},{7,6},{8,7},{9,8},{10,9},{11,1... | collective-permute-start | bytes 393224 | tf_op jit(solution)/shard_map/ppermute | solution.py:471
  38.6 23.5 %collective-permute-start = (bf16[128,512]{1,0:T(8,128)(2,1)S(1)}, bf16[128,512]{1,0:T(8,128)(2,1)S(1)}, u32[]{:S(2)}, u32[]{:S(2)}) collective-permute-start(bf16[128,512]{1,0:T(8,128)(2,1)S(1)} %get-tuple-element.33), channel_id=1, source_target_pairs={{0,1},{1,2},{2,3},{3,4},{4,5},{5,6},{6,7},{7,8},{8,9},{9,10},{10,1... | collective-permute-start | bytes 393224 | tf_op jit(solution)/shard_map/ppermute | solution.py:471
  70.4 38.5 %all-to-all-start.2 = ((bf16[128,2,8,512]{3,2,1,0:T(8,128)(2,1)}), bf16[128,2,8,512]{3,2,1,0:T(8,128)(2,1)S(1)}, u32[]{:S(2)}, u32[]{:S(2)}) async-start(bf16[128,2,8,512]{3,2,1,0:T(8,128)(2,1)} %bitcast.30), calls=%async_computation.2 | async-start | bytes 4194304 | tf_op jit(solution)/shard_map/all_to_all | solution.py:485
  77.3 23.1 %collective-permute-start.3 = (bf16[128,512]{1,0:T(8,128)(2,1)S(1)}, bf16[128,512]{1,0:T(8,128)(2,1)S(1)}, u32[]{:S(2)}, u32[]{:S(2)}) collective-permute-start(bf16[128,512]{1,0:T(8,128)(2,1)S(1)} %bitcast.23), channel_id=1, source_target_pairs={{1,0},{2,1},{3,2},{4,3},{5,4},{6,5},{7,6},{8,7},{9,8},{10,9},{11,1... | collective-permute-start | bytes 393224 | tf_op jit(solution)/shard_map/ppermute | solution.py:471
  84.4 24.4 %collective-permute-start.2 = (bf16[128,512]{1,0:T(8,128)(2,1)S(1)}, bf16[128,512]{1,0:T(8,128)(2,1)S(1)}, u32[]{:S(2)}, u32[]{:S(2)}) collective-permute-start(bf16[128,512]{1,0:T(8,128)(2,1)S(1)} %bitcast.22), channel_id=1, source_target_pairs={{0,1},{1,2},{2,3},{3,4},{4,5},{5,6},{6,7},{7,8},{8,9},{9,10},{10,1... | collective-permute-start | bytes 393224 | tf_op jit(solution)/shard_map/ppermute | solution.py:471

commit v2 on v1

v2 whole, which is shorter than its diff:
```python
import jax
import jax.numpy as jnp
from jax import lax
from jax.experimental import pallas as pl
from jax.experimental.pallas import tpu as pltpu
from jax.sharding import PartitionSpec as P

ITERS = 2
CAP = 16
GROUP = 4
AHEAD = 4
UNROLL = 8
F32 = jnp.float32
BF16 = jnp.bfloat16
VMEM = pl.BlockSpec(memory_space=pltpu.VMEM)
SMEM = pl.BlockSpec(memory_space=pltpu.SMEM)
ANY = pl.BlockSpec(memory_space=pltpu.HBM)
MIB = 1 << 20
DMA = pltpu.SemaphoreType.DMA


def in_hbm(x):
    return pltpu.with_memory_space_constraint(x, pltpu.HBM)


def in_vmem(x):
    return pltpu.with_memory_space_constraint(x, pltpu.VMEM)


def dot(a, b):
    return jnp.dot(a, b, preferred_element_type=F32)


def loop(low, high, step, unroll=1):
    def run(i, carry):
        step(i)
        return carry

    lax.fori_loop(low, high, run, 0, unroll=unroll)


def gap_sum(new, old, shape):
    gap = jnp.abs(new - old).astype(F32)
    total = jnp.zeros(shape, F32)
    for j in range(gap.shape[1] // shape[1]):
        column = gap[:, j * shape[1] : (j + 1) * shape[1]]
        total = total + jnp.sum(column.reshape(-1, *shape), axis=0)
    return total


def lane_totals(parts):
    sums = jnp.sum(parts, axis=1)
    tiles, lanes = sums.shape
    square = jnp.concatenate([sums, jnp.zeros((lanes - tiles, lanes), F32)], axis=0)
    return jnp.sum(square.T, axis=0, keepdims=True)


def pick_kernel(got_ref, cur_ref, req_ref, send_ref, flat_ref, held_ref, word_sem, in_sem, out_sem):
    slots, peers = req_ref.shape
    table = jnp.concatenate([got_ref[:, 0, :], jnp.zeros((peers, peers - slots), jnp.int32)], axis=1)
    flat_ref[...] = table.T[:8, :]
    move = pltpu.make_async_copy(flat_ref.at[pl.ds(0, slots)], req_ref, word_sem)
    move.start()
    move.wait()
    parts = in_sem.shape[0]
    batch = held_ref.shape[1] // slots
    share = held_ref.shape[0] // parts

    def fetch(i, part):
        for j in range(batch):
            for k in range(slots):
                row = req_ref[k, i * batch + j]
                pltpu.make_async_copy(cur_ref.at[row], held_ref.at[i, j * slots + k], in_sem.at[part]).start()

    for part in range(parts):
        loop(part * share, (part + 1) * share, lambda i: fetch(i, part))
    for part in range(parts):
        here = pl.ds(part * share, share)
        pltpu.make_async_copy(held_ref.at[here], held_ref.at[here], in_sem.at[part]).wait()
        pltpu.make_async_copy(held_ref.at[here], send_ref.at[here], out_sem.at[part]).start()
    for part in range(parts):
        here = pl.ds(part * share, share)
        pltpu.make_async_copy(held_ref.at[here], send_ref.at[here], out_sem.at[part]).wait()


def pick_blocks(got, blocks):
    peers, _, slots = got.shape
    shape = (peers * slots // CAP, CAP) + blocks.shape[1:]
    return pl.pallas_call(
        pick_kernel,
        out_shape=(jax.ShapeDtypeStruct((slots, peers), jnp.int32), pltpu.HBM(shape, BF16)),
        in_specs=[VMEM, ANY],
        out_specs=(SMEM, ANY),
        scratch_shapes=[pltpu.VMEM((8, peers), jnp.int32), pltpu.VMEM(shape, BF16), DMA, DMA((4,)), DMA((4,))],
        cost_estimate=pl.CostEstimate(flops=1_000_000_000, bytes_accessed=4_000_000, transcendentals=0),
        compiler_params=pltpu.CompilerParams(vmem_limit_bytes=32 * MIB),
        name="pick",
    )(in_vmem(got), in_hbm(blocks))


def prep_kernel(
    tile_ref, count_ref, seed_ref, far_ref, band_hbm,
    table_ref, aux_ref, wide_hbm, more_hbm,
    cnt_ref, num_ref, band_ref, wide_ref, more_ref, deg_ref, in_sem, out_sem, more_sem,
):
    peers = count_ref.shape[0]
    total = tile_ref.shape[0]
    slots = total // peers
    tiles, _, rows, _ = band_ref.shape
    chunks = tiles + more_ref.shape[0]
    ext_at, used_at = chunks * CAP, chunks * CAP + more_ref.shape[0]
    get_band = pltpu.make_async_copy(band_hbm, band_ref, in_sem)
    get_band.start()

    def clear(i):
        table_ref[i] = 0

    loop(0, table_ref.shape[0], clear, unroll=16)

    def clear_count(i):
        cnt_ref[i] = 0
        num_ref[i] = 0

    loop(0, chunks, clear_count, unroll=8)

    def scan(peer):
        live = count_ref[peer]
        for k in range(slots):
            @pl.when(k < live)
            def _():
                tile = tile_ref[k * peers + peer]
                place = num_ref[tile]
                num_ref[tile] = place + 1
                slot = peer * slots + k

                @pl.when(place < CAP)
                def _():
                    table_ref[tile * CAP + place] = slot

                @pl.when(place >= CAP)
                def _():
                    inner = lax.rem(place, CAP)

                    @pl.when(inner == 0)
                    def _():
                        fresh = table_ref[used_at]
                        table_ref[ext_at + fresh] = tile
                        table_ref[used_at] = fresh + 1

                    def find(c, last):
                        return jnp.where(table_ref[ext_at + c] == tile, c, last)

                    chunk = tiles + lax.fori_loop(0, table_ref[used_at], find, 0)
                    table_ref[chunk * CAP + inner] = slot
                    cnt_ref[chunk] = inner + 1

    loop(0, peers, scan, unroll=2)

    def tidy(t):
        cnt_ref[t] = jnp.minimum(num_ref[t], CAP)

    loop(0, tiles, tidy)

    def seeded(t):
        return jnp.broadcast_to(seed_ref[t].astype(F32), (rows, rows)).T == 1.0

    def weights(c):
        parts = [far_ref[table_ref[c * CAP + p]].astype(F32) for p in range(CAP)]
        mat = jnp.concatenate(parts, axis=0)
        depth = lax.broadcasted_iota(jnp.int32, mat.shape, 0)
        return jnp.where(depth < cnt_ref[c] * far_ref.shape[1], mat, 0.0).T

    get_band.wait()
    groups = tiles // GROUP

    def put_wide(g):
        here = pl.ds(g * GROUP, GROUP)
        return pltpu.make_async_copy(wide_ref.at[here], wide_hbm.at[here], out_sem.at[g])

    lane = lax.broadcasted_iota(jnp.int32, (rows, rows), 1)
    eye = (lane == lax.broadcasted_iota(jnp.int32, (rows, rows), 0)).astype(F32)

    def tile_step(t):
        seed = seeded(t)
        near = [band_ref[t, o].astype(F32) for o in range(3)]
        far = weights(t)
        degree = jnp.sum(near[0] + near[1] + near[2] + far, axis=1, keepdims=True)
        deg_ref[t] = jnp.broadcast_to(degree, (rows, rows))
        for j, (kept, other) in enumerate(zip(near + [far], (0.0, eye, 0.0, 0.0))):
            wide_ref[t, :, j * rows : (j + 1) * rows] = jnp.where(seed, other, kept).astype(BF16)

    def group_step(g):
        for i in range(GROUP):
            tile_step(g * GROUP + i)
        put_wide(g).start()

    loop(0, groups, group_step)

    def extra_step(c):
        t = table_ref[ext_at + c]
        mat = weights(tiles + c)
        more_ref[c] = jnp.where(seeded(t), 0.0, mat).astype(BF16)
        deg_ref[t] = deg_ref[t] + jnp.sum(mat, axis=1, keepdims=True)

    loop(0, table_ref[used_at], extra_step)
    put_more = pltpu.make_async_copy(more_ref, more_hbm, more_sem)
    put_more.start()
    aux_ref[...] = jnp.ones_like(aux_ref)

    def finish(t):
        cap = 1.0 / deg_ref[t] / 0.05
        aux_ref[...] = jnp.where(lane == t, jnp.where(seeded(t), -1.0, cap), aux_ref[...])

    loop(0, tiles, finish, unroll=2)
    loop(0, groups, lambda g: put_wide(g).wait())
    put_more.wait()


def prepare(far_tile, far_count, far_w, band_w, seed_rows):
    tiles, _, rows, _ = band_w.shape
    total = far_tile.shape[0]
    extra = total // CAP
    depth = CAP * far_w.shape[1]
    table = -(-((tiles + extra) * CAP + extra + 1) // 128) * 128
    wide = (tiles, rows, 3 * rows + depth)
    more = (extra, rows, depth)
    return pl.pallas_call(
        prep_kernel,
        out_shape=(
            jax.ShapeDtypeStruct((table,), jnp.int32),
            jax.ShapeDtypeStruct((rows, rows), F32),
            pltpu.HBM(wide, BF16),
            pltpu.HBM(more, BF16),
        ),
        in_specs=[SMEM, SMEM, VMEM, VMEM, ANY],
        out_specs=(SMEM, VMEM, ANY, ANY),
        scratch_shapes=[
            pltpu.SMEM((tiles + extra,), jnp.int32),
            pltpu.SMEM((tiles + extra,), jnp.int32),
            pltpu.VMEM(band_w.shape, BF16),
            pltpu.VMEM(wide, BF16),
            pltpu.VMEM(more, BF16),
            pltpu.VMEM((tiles, rows, rows), F32),
            DMA,
            DMA((tiles // GROUP,)),
            DMA,
        ],
        cost_estimate=pl.CostEstimate(flops=10_000_000_000, bytes_accessed=16_000_000, transcendentals=0),
        compiler_params=pltpu.CompilerParams(vmem_limit_bytes=32 * MIB),
        name="prep",
    )(far_tile, far_count, seed_rows, far_w, in_hbm(band_w))


def change_kernel(cur_hbm, old_hbm, res_ref, cur_ref, old_ref, part_ref, sem):
    groups = sem.shape[1]
    rows = cur_ref.shape[0] // part_ref.shape[0]
    span = cur_ref.shape[0] // groups

    def copies(g):
        here = pl.ds(g * span, span)
        return (
            pltpu.make_async_copy(cur_hbm.at[here], cur_ref.at[here], sem.at[0, g]),
            pltpu.make_async_copy(old_hbm.at[here], old_ref.at[here], sem.at[1, g]),
        )

    for g in range(groups):
        for copy in copies(g):
            copy.start()

    def step(g):
        for copy in copies(g):
            copy.wait()

        def tile(t):
            place = pl.ds(pl.multiple_of(t * rows, rows), rows)
            part_ref[t] = gap_sum(cur_ref[place, :], old_ref[place, :], part_ref.shape[1:])

        loop(g * (span // rows), (g + 1) * (span // rows), tile)

    loop(0, groups, step)
    res_ref[...] = lane_totals(part_ref[...])


def change_sums(current, old, rows, groups):
    return pl.pallas_call(
        change_kernel,
        out_shape=jax.ShapeDtypeStruct((1, rows), F32),
        in_specs=[ANY, ANY],
        out_specs=VMEM,
        scratch_shapes=[
            pltpu.VMEM(current.shape, BF16),
            pltpu.VMEM(current.shape, BF16),
            pltpu.VMEM((current.shape[0] // rows, 8, rows), F32),
            DMA((2, groups)),
        ],
        cost_estimate=pl.CostEstimate(flops=5_000_000_000, bytes_accessed=8_000_000, transcendentals=0),
        compiler_params=pltpu.CompilerParams(vmem_limit_bytes=32 * MIB),
        name="change",
    )(in_hbm(current), in_hbm(old))


def spread_kernel(first, *refs):
    if first:
        (table_ref, req_ref, aux_ref, low_ref, high_ref, recv_ref, wide_hbm, more_hbm, cur_hbm,
         new_hbm, send_hbm, top_ref, end_ref,
         wide_ref, more_ref, cur_ref, new_ref, far_ref, in_sem, more_sem, out_sem, send_ref, send_sem) = refs
    else:
        (table_ref, res_ref, aux_ref, low_ref, high_ref, recv_ref, wide_hbm, more_hbm, cur_hbm,
         new_hbm, both_ref,
         wide_ref, more_ref, cur_ref, new_ref, far_ref, in_sem, more_sem, out_sem, part_ref) = refs
    tiles, rows, width = wide_ref.shape
    extra = more_ref.shape[0]
    classes = cur_ref.shape[1]
    ext_at, used_at = (tiles + extra) * CAP, (tiles + extra) * CAP + extra
    block = new_ref.shape[1]
    per = rows // block
    groups = tiles // GROUP
    span = GROUP * rows

    def get_cur(g):
        start = pl.multiple_of(g * span, span)
        return pltpu.make_async_copy(cur_hbm.at[pl.ds(start, span)], cur_ref.at[pl.ds(start + rows, span)], in_sem.at[0, g])

    def get_wide(g):
        here = pl.ds(g * GROUP, GROUP)
        return pltpu.make_async_copy(wide_hbm.at[here], wide_ref.at[here], in_sem.at[1, g])

    def fetch(g):
        get_wide(g).start()

        @pl.when(g + 1 < groups)
        def _():
            get_cur(g + 1).start()

    get_cur(0).start()
    for g in range(AHEAD):
        fetch(g)
    get_more = pltpu.make_async_copy(more_hbm, more_ref, more_sem)

    @pl.when(table_ref[used_at] > 0)
    def _():
        get_more.start()
        get_more.wait()

    cur_ref[0:rows, :] = low_ref[...]
    cur_ref[(tiles + 1) * rows :, :] = high_ref[...]
    lane = lax.broadcasted_iota(jnp.int32, (rows, rows), 1)

    def gathered(c):
        parts = [recv_ref[table_ref[c * CAP + p]].astype(F32) for p in range(CAP)]
        return jnp.concatenate(parts, axis=0).astype(BF16)

    def put_new(g):
        here = pl.ds(g * GROUP * per, GROUP * per)
        return pltpu.make_async_copy(new_ref.at[here], new_hbm.at[here], out_sem.at[g])

    def total(t):
        near = cur_ref[pl.ds(pl.multiple_of(t * rows, rows), 3 * rows), :]
        return dot(wide_ref[t], jnp.concatenate([near, far_ref[t]], axis=0))

    def finish(t, acc):
        cap = jnp.sum(jnp.where(lane == t, aux_ref[...], 0.0), axis=1, keepdims=True)
        mean = jnp.sum(acc * acc, axis=1, keepdims=True) * (1.0 / classes)
        scale = jnp.where(cap < 0.0, 1.0, jnp.minimum(lax.rsqrt(mean), cap))
        fresh = acc * scale
        here = pl.ds(t * per, per)
        if first:
            new_ref[here] = fresh.reshape(per, block, classes).astype(BF16)
        else:
            new_ref[here] = fresh.reshape(per, block, classes).astype(BF16)
            old = cur_ref[pl.ds(pl.multiple_of((t + 1) * rows, rows), rows), :]
            part_ref[t] = gap_sum(fresh.astype(BF16), old, part_ref.shape[1:])

    def patch(t, used):
        acc = total(t)

        def add(c, acc):
            part = dot(more_ref[c], gathered(tiles + c))
            return acc + jnp.where(table_ref[ext_at + c] == t, part, 0.0)

        finish(t, lax.fori_loop(0, used, add, acc))

    def place(t):
        far_ref[t] = gathered(t)

    loop(0, tiles, place, unroll=2)
    get_cur(0).wait()

    def ready(g):
        @pl.when(g + AHEAD < groups)
        def _():
            fetch(g + AHEAD)

        get_wide(g).wait()

        @pl.when(g + 1 < groups)
        def _():
            get_cur(g + 1).wait()

    def big_step(b):
        for i in range(UNROLL // GROUP):
            ready(b * (UNROLL // GROUP) + i)

        def count(c, found):
            return found + jnp.where(lax.div(table_ref[ext_at + c], UNROLL) == b, 1, 0)

        used = table_ref[used_at]
        heavy = lax.fori_loop(0, used, count, 0) > 0

        @pl.when(jnp.logical_not(heavy))
        def _():
            for i in range(UNROLL):
                finish(b * UNROLL + i, total(b * UNROLL + i))

        @pl.when(heavy)
        def _():
            loop(b * UNROLL, (b + 1) * UNROLL, lambda t: patch(t, used))

        for i in range(UNROLL // GROUP):
            put_new(b * (UNROLL // GROUP) + i).start()

    loop(0, tiles // UNROLL, big_step)
    if first:
        slots = req_ref.shape[0]
        parts = send_sem.shape[0]
        batch = send_ref.shape[1]
        share = send_ref.shape[0] // parts

        def send_copy(part):
            here = pl.ds(part * share, share)
            return pltpu.make_async_copy(send_ref.at[here], send_hbm.at[here], send_sem.at[part])

        def choose(i):
            for j in range(batch):
                send_ref[i, j] = new_ref[req_ref[j % slots, i * (batch // slots) + j // slots]]

        for part in range(parts):
            loop(part * share, (part + 1) * share, choose)
            send_copy(part).start()
        top_ref[...] = new_ref[0:per]
        end_ref[...] = new_ref[(tiles - 1) * per :]
        for part in range(parts):
            send_copy(part).wait()
    else:
        both_ref[0:1, :] = res_ref[:, :tiles]
        both_ref[1:2, :] = lane_totals(part_ref[...])[:, :tiles]
    loop(0, groups, lambda g: put_new(g).wait())


def spread_call(first, table, side, aux, low, high, recv, wide, more, current):
    tiles, rows, _ = wide.shape
    total, block, classes = recv.shape
    blocks = pltpu.HBM((tiles * rows // block, block, classes), BF16)
    half = jax.ShapeDtypeStruct((rows // block, block, classes), BF16)
    picked = pltpu.HBM((total // CAP, CAP, block, classes), BF16)
    scratch = [
        pltpu.VMEM(wide.shape, BF16),
        pltpu.VMEM(more.shape, BF16),
        pltpu.VMEM(((tiles + 2) * rows, classes), BF16),
        pltpu.VMEM(blocks.shape, BF16),
        pltpu.VMEM((tiles, CAP * block, classes), BF16),
        DMA((2, tiles // GROUP)),
        DMA,
        DMA((tiles // GROUP,)),
    ]
    if first:
        outs, specs = (blocks, picked, half, half), (ANY, ANY, VMEM, VMEM)
        scratch += [pltpu.VMEM(picked.shape, BF16), DMA((4,))]
    else:
        outs, specs = (blocks, jax.ShapeDtypeStruct((ITERS, tiles), F32)), (ANY, VMEM)
        scratch += [pltpu.VMEM((tiles, 8, rows), F32)]
    return pl.pallas_call(
        lambda *refs: spread_kernel(first, *refs),
        out_shape=outs,
        in_specs=[SMEM, SMEM if first else VMEM] + [VMEM] * 4 + [ANY] * 3,
        out_specs=specs,
        scratch_shapes=scratch,
        cost_estimate=pl.CostEstimate(flops=4_000_000_000, bytes_accessed=18_000_000, transcendentals=0),
        compiler_params=pltpu.CompilerParams(vmem_limit_bytes=32 * MIB),
        name="spread_first" if first else "spread_last",
    )(table, side, aux, low, high, in_vmem(recv), in_hbm(wide), in_hbm(more), in_hbm(current))


def halos(first, last):
    count = lax.axis_size("node")
    forward = [(i, (i + 1) % count) for i in range(count)]
    backward = [(target, source) for source, target in forward]
    return lax.ppermute(last, "node", forward), lax.ppermute(first, "node", backward)


def body(labels, seed_mask, band_w, far_block, far_tile, far_count, far_w):
    node_rows, classes = labels.shape
    tiles, _, rows, _ = band_w.shape
    _, peers, slots, block, _ = far_w.shape
    total = peers * slots
    got = lax.all_to_all(far_block, "node", split_axis=1, concat_axis=0, tiled=True)
    blocks = labels.reshape(-1, block, classes)
    requests, send = pick_blocks(got, blocks)

    def exchange(x):
        x = x.reshape(peers, slots, block, classes)
        return lax.all_to_all(x, "node", split_axis=0, concat_axis=0, tiled=True).reshape(total, block, classes)

    recv = exchange(send)
    low, high = halos(labels[:rows], labels[-rows:])
    table, aux, wide, more = prepare(
        far_tile[0].T.reshape(total), far_count[0], far_w.reshape(total, block, rows), band_w, seed_mask.reshape(tiles, 1, rows)
    )
    new, send, top, end = spread_call(True, table, requests, aux, low, high, recv, wide, more, labels)
    recv = exchange(send)
    low, high = halos(top.reshape(rows, classes), end.reshape(rows, classes))
    current = new.reshape(node_rows, classes)
    change = change_sums(current, labels, rows, tiles // GROUP)
    final, both = spread_call(False, table, change, aux, low, high, recv, wide, more, current)
    return final.reshape(node_rows, classes), both


def solution(mesh):
    placed = (
        P("node", None),
        P("node"),
        P("node", None, None, None),
        P("node", None, None),
        P("node", None, None),
        P("node", None),
        P("node", None, None, None, None),
    )
    return jax.shard_map(
        body,
        mesh=mesh,
        in_specs=placed,
        out_specs=(P("node", None), P(None, "node")),
        check_vma=False,
    )
```

time: 119 us -> 115 us (0.966)
  Pallas kernels: 56.5 us -> 32.9 us
  waiting for transfers between devices: 13.8 us -> 34.3 us
    ppermute x2, waiting for transfers between devices: 10.6 us -> 29 us  [halos(): lax.ppermute(last, 'node', forward)]
    pallas_call x3, Pallas kernels: 31.2 us -> 19.2 us  [the longest x2 15.4 us: spread_call(): pl.pallas_call(lambda *refs: spread_kernel(first, *refs), out_shape=outs,...]
    pallas_call x1, Pallas kernels: 21.2 us -> 9.63 us  [prepare(): pl.pallas_call(prep_kernel, out_shape=(jax.ShapeDtypeStruct((table,), jnp...]
    ppermute x2, waiting for transfers between devices: 3.19 us -> 5.32 us  [halos(): lax.ppermute(first, 'node', backward)]
  transfers between devices with their start and end apart: 6 -> 6, of which waited for: 3 -> 3; matrix products, arithmetic and copies ran while one was open for 1% -> 1% of each run, Pallas kernels for 29% -> 12%
where the time goes in v2:
time: 115 us
  waiting for transfers between devices  34.3 us (30%)
  Pallas kernels  32.9 us (29%)
  starting transfers between devices  25.4 us (22%)
  blocking collectives  20.3 us (18%)
  local copies, waits for them, and re-layouts  1.79 us (2%)
    ppermute x2, waiting for transfers between devices, halos(): lax.ppermute(last, 'node', forward)  29 us
    all_to_all x1, blocking collectives, body(): lax.all_to_all(far_block, 'node', split_axis=1, concat_axis=0, tiled=True)  20.3 us
    pallas_call x2, Pallas kernels, spread_call(): pl.pallas_call(lambda *refs: spread_kernel(first, *refs), out_shape=outs,...  15.4 us
    ppermute x2, starting transfers between devices, halos(): lax.ppermute(first, 'node', backward)  14.3 us
    all_to_all x2, starting transfers between devices, exchange(): lax.all_to_all(x, 'node', split_axis=0, concat_axis=0, tiled=True)  11.1 us
    pallas_call x1, Pallas kernels, prepare(): pl.pallas_call(prep_kernel, out_shape=(jax.ShapeDtypeStruct((table,), jnp...  9.63 us
    ppermute x2, waiting for transfers between devices, halos(): lax.ppermute(first, 'node', backward)  5.32 us
    pallas_call x1, Pallas kernels, pick_blocks(): pl.pallas_call(pick_kernel, out_shape=(jax.ShapeDtypeStruct((slots, peers...  4.04 us
  transfers between devices with their start and end apart: 6, of which 3 were waited for; matrix products, arithmetic and copies ran while one was open for 1% of the time, Pallas kernels for 12%

profile of v2, /device:TPU:0, one launch (start us, length us, event | category | flops | bytes accessed | tf_op | source)
XLA Modules:
  0.0 115.4 jit_solution(9658792296808647469)
XLA Ops:
  0.6 0.8 copy.10
  1.4 20.3 %all_to_all.22 = s32[1,128,2]{2,0,1:T(1,128)S(1)} all-to-all(s32[1,128,2]{2,0,1:T(1,128)S(1)} %copy.10), channel_id=1, replica_groups=mesh['node'=128] {'node'}, dimensions={1} | all-to-all | bytes 2048 | tf_op jit(solution)/shard_map/all_to_all | solution.py:496
  21.7 4.0 %pick.1 = (s32[2,128]{1,0:T(2,128)S(1)}, bf16[16,16,8,512]{3,2,1,0:T(8,128)(2,1)}) custom-call(s32[128,1,2]{2,1,0:T(1,128)S(1)} %bitcast.20, bf16[512,8,512]{2,1,0:T(8,128)(2,1)} %bitcast.27), custom_call_target="tpu_custom_call" | custom-call | flops 1000000000 | bytes 4000000 | tf_op jit(solution)/shard_map/pick/pallas_call | solution.py:89
  25.8 4.7 %all-to-all-start.1 = ((bf16[128,2,8,512]{3,2,1,0:T(8,128)(2,1)}), bf16[128,2,8,512]{3,2,1,0:T(8,128)(2,1)S(1)}, u32[]{:S(2)}, u32[]{:S(2)}) async-start(bf16[128,2,8,512]{3,2,1,0:T(8,128)(2,1)} %bitcast.28), calls=%async_computation.1 | async-start | bytes 4194304 | tf_op jit(solution)/shard_map/all_to_all | solution.py:502
  30.5 1.0 fusion
  31.5 7.1 %collective-permute-start.1 = (bf16[128,512]{1,0:T(8,128)(2,1)S(1)}, bf16[128,512]{1,0:T(8,128)(2,1)S(1)}, u32[]{:S(2)}, u32[]{:S(2)}) collective-permute-start(bf16[128,512]{1,0:T(8,128)(2,1)S(1)} %get-tuple-element.26), channel_id=1, source_target_pairs={{1,0},{2,1},{3,2},{4,3},{5,4},{6,5},{7,6},{8,7},{9,8},{10,9},{11,1... | collective-permute-start | bytes 393224 | tf_op jit(solution)/shard_map/ppermute | solution.py:488
  38.6 0.0 collective-permute-start
  38.6 0.0 copy-done
  38.6 0.0 copy-done.1
  38.6 0.0 copy-done.2
  38.6 0.0 copy-done.3
  38.6 9.6 %prep.1 = (s32[896]{0:T(1024)S(1)}, f32[128,128]{1,0:T(8,128)S(1)}, bf16[32,128,512]{2,1,0:T(8,128)(2,1)}, bf16[16,128,128]{2,1,0:T(8,128)(2,1)}) custom-call(s32[256]{0:T(256)S(1)} %bitcast.25, s32[128]{0:T(128)S(1)} %bitcast.26, s32[32,1,128]{2,1,0:T(1,128)S(1)} %bitcast.24, bf16[256,8,128]{2,1,0:T(8,128)(2,1)S(1)} %bitcast.21, ...), custom_call_target="tpu_custom_call" | custom-call | flops 10000000000 | bytes 16000000 | tf_op jit(solution)/shard_map/prep/pallas_call | solution.py:227
  48.3 5.3 %collective-permute-done.1.refs_4_ = bf16[128,512]{1,0:T(8,128)(2,1)S(1)} collective-permute-done((bf16[128,512]{1,0:T(8,128)(2,1)S(1)}, bf16[128,512]{1,0:T(8,128)(2,1)S(1)}, u32[]{:S(2)}, u32[]{:S(2)}) %collective-permute-start.1) | collective-permute-done | bytes 131104 | tf_op jit(solution)/shard_map/ppermute | solution.py:488
  53.6 8.5 %collective-permute-done.refs_3_ = bf16[128,512]{1,0:T(8,128)(2,1)S(1)} collective-permute-done((bf16[128,512]{1,0:T(8,128)(2,1)S(1)}, bf16[128,512]{1,0:T(8,128)(2,1)S(1)}, u32[]{:S(2)}, u32[]{:S(2)}) %collective-permute-start) | collective-permute-done | bytes 131104 | tf_op jit(solution)/shard_map/ppermute | solution.py:488
  62.0 0.0 all-to-all-done.1
  62.0 7.7 %spread_first.1 = (bf16[512,8,512]{2,1,0:T(8,128)(2,1)}, bf16[16,16,8,512]{3,2,1,0:T(8,128)(2,1)}, bf16[16,8,512]{2,1,0:T(8,128)(2,1)S(1)}, bf16[16,8,512]{2,1,0:T(8,128)(2,1)S(1)}) custom-call(s32[896]{0:T(1024)S(1)} %get-tuple-element.14.refs_0_, s32[2,128]{1,0:T(2,128)S(1)} %get-tuple-element.15.refs_1_, f32[128,128]{1,0:T(8,128)S(1)} %get-tuple-element.16.refs_2_, ...), custom_call_target="tpu_custom_call" | custom-call | flops 4000000000 | bytes 18000000 | tf_op jit(solution)/shard_map/spread_first/pallas_call | solution.py:472
  69.8 6.4 %all-to-all-start.2 = ((bf16[128,2,8,512]{3,2,1,0:T(8,128)(2,1)}), bf16[128,2,8,512]{3,2,1,0:T(8,128)(2,1)S(1)}, u32[]{:S(2)}, u32[]{:S(2)}) async-start(bf16[128,2,8,512]{3,2,1,0:T(8,128)(2,1)} %bitcast.29), calls=%async_computation.2 | async-start | bytes 4194304 | tf_op jit(solution)/shard_map/all_to_all | solution.py:502
  76.1 0.1 collective-permute-start.2
  76.2 7.2 %collective-permute-start.3 = (bf16[128,512]{1,0:T(8,128)(2,1)S(1)}, bf16[128,512]{1,0:T(8,128)(2,1)S(1)}, u32[]{:S(2)}, u32[]{:S(2)}) collective-permute-start(bf16[128,512]{1,0:T(8,128)(2,1)S(1)} %bitcast.22), channel_id=1, source_target_pairs={{1,0},{2,1},{3,2},{4,3},{5,4},{6,5},{7,6},{8,7},{9,8},{10,9},{11,1... | collective-permute-start | bytes 393224 | tf_op jit(solution)/shard_map/ppermute | solution.py:488
  83.4 3.8 %change.1.refs_1_ = f32[1,128]{1,0:T(1,128)S(1)} custom-call(bf16[4096,512]{1,0:T(8,128)(2,1)} %bitcast.30, bf16[4096,512]{1,0:T(8,128)(2,1)} %old_hbm.1), custom_call_target="tpu_custom_call" | custom-call | flops 5000000000 | bytes 8000000 | tf_op jit(solution)/shard_map/change/pallas_call | solution.py:285
  87.2 20.5 %collective-permute-done.2.refs_3_ = bf16[128,512]{1,0:T(8,128)(2,1)S(1)} collective-permute-done((bf16[128,512]{1,0:T(8,128)(2,1)S(1)}, bf16[128,512]{1,0:T(8,128)(2,1)S(1)}, u32[]{:S(2)}, u32[]{:S(2)}) %collective-permute-start.2) | collective-permute-done | bytes 131104 | tf_op jit(solution)/shard_map/ppermute | solution.py:488
  107.7 0.0 collective-permute-done.3.refs_4_
  107.7 0.0 all-to-all-done.2
  107.7 7.7 %spread_last.1 = (bf16[512,8,512]{2,1,0:T(8,128)(2,1)}, f32[2,32]{1,0:T(2,128)}) custom-call(s32[896]{0:T(1024)S(1)} %get-tuple-element.14.refs_0_, f32[1,128]{1,0:T(1,128)S(1)} %change.1.refs_1_, f32[128,128]{1,0:T(8,128)S(1)} %get-tuple-element.16.refs_2_, bf16[128,512]{1,0:T(8,128)(2,1)S(1)} %collective-permute-done.2.refs_3_, ...), custom_call_target="tpu_custom_call" | custom-call | flops 4000000000 | bytes 18000000 | tf_op jit(solution)/shard_map/spread_last/pallas_call | solution.py:472
  (4 shorter events, 0.0 us)
Async XLA Ops:
  21.7 16.9 %copy-start = (bf16[1,128,2,8,128]{4,3,2,1,0:T(8,128)(2,1)S(1)}, bf16[1,128,2,8,128]{4,3,2,1,0:T(8,128)(2,1)}, u32[]{:S(2)}) copy-start(bf16[1,128,2,8,128]{4,3,2,1,0:T(8,128)(2,1)} %param.13) | copy-start | bytes 1572868
  21.7 16.9 %copy-start.1 = (s32[4096]{0:T(1024)S(1)}, s32[4096]{0:T(1024)}, u32[]{:S(2)}) copy-start(s32[4096]{0:T(1024)} %param.8) | copy-start | bytes 49156
  21.7 16.9 %copy-start.2 = (s32[1,128,2]{1,2,0:T(2,128)S(1)}, s32[1,128,2]{1,2,0:T(2,128)}, u32[]{:S(2)}) copy-start(s32[1,128,2]{1,2,0:T(2,128)} %param.11) | copy-start | bytes 3076
  21.7 16.9 %copy-start.3 = (s32[1,128]{1,0:T(1,128)S(1)}, s32[1,128]{1,0:T(1,128)}, u32[]{:S(2)}) copy-start(s32[1,128]{1,0:T(1,128)} %param.12) | copy-start | bytes 1540
  25.8 36.3 %all-to-all-start.1 = ((bf16[128,2,8,512]{3,2,1,0:T(8,128)(2,1)}), bf16[128,2,8,512]{3,2,1,0:T(8,128)(2,1)S(1)}, u32[]{:S(2)}, u32[]{:S(2)}) async-start(bf16[128,2,8,512]{3,2,1,0:T(8,128)(2,1)} %bitcast.28), calls=%async_computation.1 | async-start | bytes 4194304 | tf_op jit(solution)/shard_map/all_to_all | solution.py:502
  31.5 22.1 %collective-permute-start.1 = (bf16[128,512]{1,0:T(8,128)(2,1)S(1)}, bf16[128,512]{1,0:T(8,128)(2,1)S(1)}, u32[]{:S(2)}, u32[]{:S(2)}) collective-permute-start(bf16[128,512]{1,0:T(8,128)(2,1)S(1)} %get-tuple-element.26), channel_id=1, source_target_pairs={{1,0},{2,1},{3,2},{4,3},{5,4},{6,5},{7,6},{8,7},{9,8},{10,9},{11,1... | collective-permute-start | bytes 393224 | tf_op jit(solution)/shard_map/ppermute | solution.py:488
  38.6 23.5 %collective-permute-start = (bf16[128,512]{1,0:T(8,128)(2,1)S(1)}, bf16[128,512]{1,0:T(8,128)(2,1)S(1)}, u32[]{:S(2)}, u32[]{:S(2)}) collective-permute-start(bf16[128,512]{1,0:T(8,128)(2,1)S(1)} %get-tuple-element.27), channel_id=1, source_target_pairs={{0,1},{1,2},{2,3},{3,4},{4,5},{5,6},{6,7},{7,8},{8,9},{9,10},{10,1... | collective-permute-start | bytes 393224 | tf_op jit(solution)/shard_map/ppermute | solution.py:488
  69.8 37.9 %all-to-all-start.2 = ((bf16[128,2,8,512]{3,2,1,0:T(8,128)(2,1)}), bf16[128,2,8,512]{3,2,1,0:T(8,128)(2,1)S(1)}, u32[]{:S(2)}, u32[]{:S(2)}) async-start(bf16[128,2,8,512]{3,2,1,0:T(8,128)(2,1)} %bitcast.29), calls=%async_computation.2 | async-start | bytes 4194304 | tf_op jit(solution)/shard_map/all_to_all | solution.py:502
  76.1 31.5 %collective-permute-start.2 = (bf16[128,512]{1,0:T(8,128)(2,1)S(1)}, bf16[128,512]{1,0:T(8,128)(2,1)S(1)}, u32[]{:S(2)}, u32[]{:S(2)}) collective-permute-start(bf16[128,512]{1,0:T(8,128)(2,1)S(1)} %bitcast.23), channel_id=1, source_target_pairs={{0,1},{1,2},{2,3},{3,4},{4,5},{5,6},{6,7},{7,8},{8,9},{9,10},{10,1... | collective-permute-start | bytes 393224 | tf_op jit(solution)/shard_map/ppermute | solution.py:488
  76.2 31.5 %collective-permute-start.3 = (bf16[128,512]{1,0:T(8,128)(2,1)S(1)}, bf16[128,512]{1,0:T(8,128)(2,1)S(1)}, u32[]{:S(2)}, u32[]{:S(2)}) collective-permute-start(bf16[128,512]{1,0:T(8,128)(2,1)S(1)} %bitcast.22), channel_id=1, source_target_pairs={{1,0},{2,1},{3,2},{4,3},{5,4},{6,5},{7,6},{8,7},{9,8},{10,9},{11,1... | collective-permute-start | bytes 393224 | tf_op jit(solution)/shard_map/ppermute | solution.py:488

commit v3 on v2

--- a/solution.py
+++ b/solution.py
@@ -55,13 +55,15 @@
     return jnp.sum(square.T, axis=0, keepdims=True)
 
 
-def pick_kernel(got_ref, cur_ref, req_ref, send_ref, flat_ref, held_ref, word_sem, in_sem, out_sem):
+def pick_kernel(got_ref, cur_ref, req_hbm, send_ref, flat_ref, req_ref, held_ref, word_sem, in_sem, out_sem):
     slots, peers = req_ref.shape
     table = jnp.concatenate([got_ref[:, 0, :], jnp.zeros((peers, peers - slots), jnp.int32)], axis=1)
     flat_ref[...] = table.T[:8, :]
     move = pltpu.make_async_copy(flat_ref.at[pl.ds(0, slots)], req_ref, word_sem)
     move.start()
     move.wait()
+    keep = pltpu.make_async_copy(req_ref, req_hbm, word_sem)
+    keep.start()
     parts = in_sem.shape[0]
     batch = held_ref.shape[1] // slots
     share = held_ref.shape[0] // parts
@@ -81,6 +83,7 @@
     for part in range(parts):
         here = pl.ds(part * share, share)
         pltpu.make_async_copy(held_ref.at[here], send_ref.at[here], out_sem.at[part]).wait()
+    keep.wait()
 
 
 def pick_blocks(got, blocks):
@@ -88,10 +91,17 @@
     shape = (peers * slots // CAP, CAP) + blocks.shape[1:]
     return pl.pallas_call(
         pick_kernel,
-        out_shape=(jax.ShapeDtypeStruct((slots, peers), jnp.int32), pltpu.HBM(shape, BF16)),
+        out_shape=(pltpu.HBM((slots, peers), jnp.int32), pltpu.HBM(shape, BF16)),
         in_specs=[VMEM, ANY],
-        out_specs=(SMEM, ANY),
-        scratch_shapes=[pltpu.VMEM((8, peers), jnp.int32), pltpu.VMEM(shape, BF16), DMA, DMA((4,)), DMA((4,))],
+        out_specs=(ANY, ANY),
+        scratch_shapes=[
+            pltpu.VMEM((8, peers), jnp.int32),
+            pltpu.SMEM((slots, peers), jnp.int32),
+            pltpu.VMEM(shape, BF16),
+            DMA,
+            DMA((4,)),
+            DMA((4,)),
+        ],
         cost_estimate=pl.CostEstimate(flops=1_000_000_000, bytes_accessed=4_000_000, transcendentals=0),
         compiler_params=pltpu.CompilerParams(vmem_limit_bytes=32 * MIB),
         name="pick",
@@ -100,8 +110,8 @@
 
 def prep_kernel(
     tile_ref, count_ref, seed_ref, far_ref, band_hbm,
-    table_ref, aux_ref, wide_hbm, more_hbm,
-    cnt_ref, num_ref, band_ref, wide_ref, more_ref, deg_ref, in_sem, out_sem, more_sem,
+    table_hbm, aux_ref, wide_hbm, more_hbm,
+    table_ref, cnt_ref, num_ref, band_ref, wide_ref, more_ref, deg_ref, in_sem, out_sem, more_sem, table_sem,
 ):
     peers = count_ref.shape[0]
     total = tile_ref.shape[0]
@@ -156,6 +166,9 @@
 
     loop(0, peers, scan, unroll=2)
 
+    put_table = pltpu.make_async_copy(table_ref, table_hbm, table_sem)
+    put_table.start()
+
     def tidy(t):
         cnt_ref[t] = jnp.minimum(num_ref[t], CAP)
 
@@ -214,6 +227,7 @@
     loop(0, tiles, finish, unroll=2)
     loop(0, groups, lambda g: put_wide(g).wait())
     put_more.wait()
+    put_table.wait()
 
 
 def prepare(far_tile, far_count, far_w, band_w, seed_rows):
@@ -227,14 +241,15 @@
     return pl.pallas_call(
         prep_kernel,
         out_shape=(
-            jax.ShapeDtypeStruct((table,), jnp.int32),
+            pltpu.HBM((table,), jnp.int32),
             jax.ShapeDtypeStruct((rows, rows), F32),
             pltpu.HBM(wide, BF16),
             pltpu.HBM(more, BF16),
         ),
         in_specs=[SMEM, SMEM, VMEM, VMEM, ANY],
-        out_specs=(SMEM, VMEM, ANY, ANY),
+        out_specs=(ANY, VMEM, ANY, ANY),
         scratch_shapes=[
+            pltpu.SMEM((table,), jnp.int32),
             pltpu.SMEM((tiles + extra,), jnp.int32),
             pltpu.SMEM((tiles + extra,), jnp.int32),
             pltpu.VMEM(band_w.shape, BF16),
@@ -243,6 +258,7 @@
             pltpu.VMEM((tiles, rows, rows), F32),
             DMA,
             DMA((tiles // GROUP,)),
+            DMA,
             DMA,
         ],
         cost_estimate=pl.CostEstimate(flops=10_000_000_000, bytes_accessed=16_000_000, transcendentals=0),
@@ -301,13 +317,15 @@
 
 def spread_kernel(first, *refs):
     if first:
-        (table_ref, req_ref, aux_ref, low_ref, high_ref, recv_ref, wide_hbm, more_hbm, cur_hbm,
+        (table_hbm, req_hbm, aux_ref, low_ref, high_ref, recv_ref, wide_hbm, more_hbm, cur_hbm,
          new_hbm, send_hbm, top_ref, end_ref,
-         wide_ref, more_ref, cur_ref, new_ref, far_ref, in_sem, more_sem, out_sem, send_ref, send_sem) = refs
+         table_ref, wide_ref, more_ref, cur_ref, new_ref, far_ref, in_sem, more_sem, out_sem, table_sem,
+         req_ref, side_sem, send_ref, send_sem) = refs
     else:
-        (table_ref, res_ref, aux_ref, low_ref, high_ref, recv_ref, wide_hbm, more_hbm, cur_hbm,
-         new_hbm, both_ref,
-         wide_ref, more_ref, cur_ref, new_ref, far_ref, in_sem, more_sem, out_sem, part_ref) = refs
+        (table_hbm, res_ref, aux_ref, low_ref, high_ref, recv_ref, wide_hbm, more_hbm, cur_hbm,
+         new_hbm, both_hbm,
+         table_ref, wide_ref, more_ref, cur_ref, new_ref, far_ref, in_sem, more_sem, out_sem, table_sem,
+         both_ref, side_sem, part_ref) = refs
     tiles, rows, width = wide_ref.shape
     extra = more_ref.shape[0]
     classes = cur_ref.shape[1]
@@ -332,9 +350,17 @@
         def _():
             get_cur(g + 1).start()
 
+    get_table = pltpu.make_async_copy(table_hbm, table_ref, table_sem)
+    get_table.start()
+    if first:
+        get_req = pltpu.make_async_copy(req_hbm, req_ref, side_sem)
+        get_req.start()
     get_cur(0).start()
     for g in range(AHEAD):
         fetch(g)
+    cur_ref[0:rows, :] = low_ref[...]
+    cur_ref[(tiles + 1) * rows :, :] = high_ref[...]
+    get_table.wait()
     get_more = pltpu.make_async_copy(more_hbm, more_ref, more_sem)
 
     @pl.when(table_ref[used_at] > 0)
@@ -342,8 +368,6 @@
         get_more.start()
         get_more.wait()
 
-    cur_ref[0:rows, :] = low_ref[...]
-    cur_ref[(tiles + 1) * rows :, :] = high_ref[...]
     lane = lax.broadcasted_iota(jnp.int32, (rows, rows), 1)
 
     def gathered(c):
@@ -401,26 +425,29 @@
         for i in range(UNROLL // GROUP):
             ready(b * (UNROLL // GROUP) + i)
 
-        def count(c, found):
-            return found + jnp.where(lax.div(table_ref[ext_at + c], UNROLL) == b, 1, 0)
-
+        for i in range(UNROLL):
+            finish(b * UNROLL + i, total(b * UNROLL + i))
+            if i % GROUP == GROUP - 1:
+                put_new(b * (UNROLL // GROUP) + i // GROUP).start()
         used = table_ref[used_at]
-        heavy = lax.fori_loop(0, used, count, 0) > 0
-
-        @pl.when(jnp.logical_not(heavy))
-        def _():
-            for i in range(UNROLL):
-                finish(b * UNROLL + i, total(b * UNROLL + i))
-
-        @pl.when(heavy)
-        def _():
-            loop(b * UNROLL, (b + 1) * UNROLL, lambda t: patch(t, used))
-
-        for i in range(UNROLL // GROUP):
-            put_new(b * (UNROLL // GROUP) + i).start()
+
+        def redo(c):
+            t = table_ref[ext_at + c]
+
+            def same(k, hits):
+                return hits + jnp.where(table_ref[ext_at + k] == t, 1, 0)
+
+            @pl.when((lax.div(t, UNROLL) == b) & (lax.fori_loop(0, c, same, 0) == 0))
+            def _():
+                put_new(lax.div(t, GROUP)).wait()
+                patch(t, used)
+                put_new(lax.div(t, GROUP)).start()
+
+        loop(0, used, redo)
 
     loop(0, tiles // UNROLL, big_step)
     if first:
+        get_req.wait()
         slots = req_ref.shape[0]
         parts = send_sem.shape[0]
         batch = send_ref.shape[1]
@@ -444,6 +471,9 @@
     else:
         both_ref[0:1, :] = res_ref[:, :tiles]
         both_ref[1:2, :] = lane_totals(part_ref[...])[:, :tiles]
+        put_both = pltpu.make_async_copy(both_ref, both_hbm, side_sem)
+        put_both.start()
+        put_both.wait()
     loop(0, groups, lambda g: put_new(g).wait())
 
 
@@ -454,6 +484,7 @@
     half = jax.ShapeDtypeStruct((rows // block, block, classes), BF16)
     picked = pltpu.HBM((total // CAP, CAP, block, classes), BF16)
     scratch = [
+        pltpu.SMEM(table.shape, jnp.int32),
         pltpu.VMEM(wide.shape, BF16),
         pltpu.VMEM(more.shape, BF16),
         pltpu.VMEM(((tiles + 2) * rows, classes), BF16),
@@ -462,23 +493,25 @@
         DMA((2, tiles // GROUP)),
         DMA,
         DMA((tiles // GROUP,)),
+        DMA,
     ]
     if first:
         outs, specs = (blocks, picked, half, half), (ANY, ANY, VMEM, VMEM)
-        scratch += [pltpu.VMEM(picked.shape, BF16), DMA((4,))]
+        scratch += [pltpu.SMEM(side.shape, jnp.int32), DMA, pltpu.VMEM(picked.shape, BF16), DMA((8,))]
+        side = in_hbm(side)
     else:
-        outs, specs = (blocks, jax.ShapeDtypeStruct((ITERS, tiles), F32)), (ANY, VMEM)
-        scratch += [pltpu.VMEM((tiles, 8, rows), F32)]
+        outs, specs = (blocks, pltpu.HBM((ITERS, tiles), F32)), (ANY, ANY)
+        scratch += [pltpu.VMEM((ITERS, tiles), F32), DMA, pltpu.VMEM((tiles, 8, rows), F32)]
     return pl.pallas_call(
         lambda *refs: spread_kernel(first, *refs),
         out_shape=outs,
-        in_specs=[SMEM, SMEM if first else VMEM] + [VMEM] * 4 + [ANY] * 3,
+        in_specs=[ANY, ANY if first else VMEM] + [VMEM] * 4 + [ANY] * 3,
         out_specs=specs,
         scratch_shapes=scratch,
         cost_estimate=pl.CostEstimate(flops=4_000_000_000, bytes_accessed=18_000_000, transcendentals=0),
         compiler_params=pltpu.CompilerParams(vmem_limit_bytes=32 * MIB),
         name="spread_first" if first else "spread_last",
-    )(table, side, aux, low, high, in_vmem(recv), in_hbm(wide), in_hbm(more), in_hbm(current))
+    )(in_hbm(table), side, aux, low, high, in_vmem(recv), in_hbm(wide), in_hbm(more), in_hbm(current))
 
 
 def halos(first, last):

time: 115 us -> 112 us (0.974); the launches traced: 115 us -> 111 us
  Pallas kernels: 32.9 us -> 29.8 us
  starting transfers between devices: 25.4 us -> 23.7 us
    pallas_call x2, Pallas kernels: 15.4 us -> 13.3 us  [spread_call(): pl.pallas_call(lambda *refs: spread_kernel(first, *refs), out_shape=outs,...]
    all_to_all x2, starting transfers between devices: 11.1 us -> 9.34 us  [exchange(): lax.all_to_all(x, 'node', split_axis=0, concat_axis=0, tiled=True)]
where the time goes in v3:
time: 112 us; the launch traced here: 111 us
  waiting for transfers between devices  34.9 us (31%)
  Pallas kernels  29.8 us (27%)
  starting transfers between devices  23.7 us (21%)
  blocking collectives  20.3 us (18%)
  local copies, waits for them, and re-layouts  1.79 us (2%)
    ppermute x2, waiting for transfers between devices, halos(): lax.ppermute(last, 'node', forward)  29.1 us
    all_to_all x1, blocking collectives, body(): lax.all_to_all(far_block, 'node', split_axis=1, concat_axis=0, tiled=True)  20.3 us
    ppermute x2, starting transfers between devices, halos(): lax.ppermute(first, 'node', backward)  14.3 us
    pallas_call x2, Pallas kernels, spread_call(): pl.pallas_call(lambda *refs: spread_kernel(first, *refs), out_shape=outs,...  13.3 us
    all_to_all x2, starting transfers between devices, exchange(): lax.all_to_all(x, 'node', split_axis=0, concat_axis=0, tiled=True)  9.34 us
    pallas_call x1, Pallas kernels, prepare(): pl.pallas_call(prep_kernel, out_shape=(pltpu.HBM((table,), jnp.int32), ja...  9.07 us
    ppermute x2, waiting for transfers between devices, halos(): lax.ppermute(first, 'node', backward)  5.75 us
    pallas_call x1, Pallas kernels, change_sums(): pl.pallas_call(change_kernel, out_shape=jax.ShapeDtypeStruct((1, rows), F...  3.79 us
  transfers between devices with their start and end apart: 6, of which 3 were waited for; matrix products, arithmetic and copies ran while one was open for 1% of the time, Pallas kernels for 12%

profile of v3, /device:TPU:0, one launch (start us, length us, event | category | flops | bytes accessed | tf_op | source)
XLA Modules:
  0.0 111.2 jit_solution(18282590932528308044)
XLA Ops:
  0.6 0.8 copy.10
  1.4 20.3 %all_to_all.22 = s32[1,128,2]{2,0,1:T(1,128)S(1)} all-to-all(s32[1,128,2]{2,0,1:T(1,128)S(1)} %copy.10), channel_id=1, replica_groups=mesh['node'=128] {'node'}, dimensions={1} | all-to-all | bytes 2048 | tf_op jit(solution)/shard_map/all_to_all | solution.py:529
  21.7 3.6 %pick.1 = (s32[2,128]{1,0:T(2,128)}, bf16[16,16,8,512]{3,2,1,0:T(8,128)(2,1)}) custom-call(s32[128,1,2]{2,1,0:T(1,128)S(1)} %bitcast.20, bf16[512,8,512]{2,1,0:T(8,128)(2,1)} %bitcast.27), custom_call_target="tpu_custom_call" | custom-call | flops 1000000000 | bytes 4000000 | tf_op jit(solution)/shard_map/pick/pallas_call | solution.py:92
  25.4 4.7 %all-to-all-start.1 = ((bf16[128,2,8,512]{3,2,1,0:T(8,128)(2,1)}), bf16[128,2,8,512]{3,2,1,0:T(8,128)(2,1)S(1)}, u32[]{:S(2)}, u32[]{:S(2)}) async-start(bf16[128,2,8,512]{3,2,1,0:T(8,128)(2,1)} %bitcast.28), calls=%async_computation.1 | async-start | bytes 4194304 | tf_op jit(solution)/shard_map/all_to_all | solution.py:535
  30.0 1.0 fusion
  31.0 7.1 %collective-permute-start.1 = (bf16[128,512]{1,0:T(8,128)(2,1)S(1)}, bf16[128,512]{1,0:T(8,128)(2,1)S(1)}, u32[]{:S(2)}, u32[]{:S(2)}) collective-permute-start(bf16[128,512]{1,0:T(8,128)(2,1)S(1)} %get-tuple-element.26), channel_id=1, source_target_pairs={{1,0},{2,1},{3,2},{4,3},{5,4},{6,5},{7,6},{8,7},{9,8},{10,9},{11,1... | collective-permute-start | bytes 393224 | tf_op jit(solution)/shard_map/ppermute | solution.py:521
  38.1 0.0 collective-permute-start
  38.1 0.0 copy-done
  38.1 0.0 copy-done.1
  38.1 0.0 copy-done.2
  38.1 0.0 copy-done.3
  38.2 9.1 %prep.1 = (s32[896]{0:T(1024)}, f32[128,128]{1,0:T(8,128)S(1)}, bf16[32,128,512]{2,1,0:T(8,128)(2,1)}, bf16[16,128,128]{2,1,0:T(8,128)(2,1)}) custom-call(s32[256]{0:T(256)S(1)} %bitcast.25, s32[128]{0:T(128)S(1)} %bitcast.26, s32[32,1,128]{2,1,0:T(1,128)S(1)} %bitcast.24, bf16[256,8,128]{2,1,0:T(8,128)(2,1)S(1)} %bitcast.21, bf16[32,3,128,128]{3,2,1,0:T(8,128)(2,1)} %band_hbm.1), custom_call_target="tpu_custom_call" | custom-call | flops 10000000000 | bytes 16000000 | tf_op jit(solution)/shard_map/prep/pallas_call | solution.py:241
  47.2 5.8 %collective-permute-done.1.refs_4_ = bf16[128,512]{1,0:T(8,128)(2,1)S(1)} collective-permute-done((bf16[128,512]{1,0:T(8,128)(2,1)S(1)}, bf16[128,512]{1,0:T(8,128)(2,1)S(1)}, u32[]{:S(2)}, u32[]{:S(2)}) %collective-permute-start.1) | collective-permute-done | bytes 131104 | tf_op jit(solution)/shard_map/ppermute | solution.py:521
  53.0 8.6 %collective-permute-done.refs_3_ = bf16[128,512]{1,0:T(8,128)(2,1)S(1)} collective-permute-done((bf16[128,512]{1,0:T(8,128)(2,1)S(1)}, bf16[128,512]{1,0:T(8,128)(2,1)S(1)}, u32[]{:S(2)}, u32[]{:S(2)}) %collective-permute-start) | collective-permute-done | bytes 131104 | tf_op jit(solution)/shard_map/ppermute | solution.py:521
  61.6 0.0 all-to-all-done.1
  61.6 7.0 %spread_first.1 = (bf16[512,8,512]{2,1,0:T(8,128)(2,1)}, bf16[16,16,8,512]{3,2,1,0:T(8,128)(2,1)}, bf16[16,8,512]{2,1,0:T(8,128)(2,1)S(1)}, bf16[16,8,512]{2,1,0:T(8,128)(2,1)S(1)}) custom-call(s32[896]{0:T(1024)} %get-tuple-element.14.refs_0_, s32[2,128]{1,0:T(2,128)} %get-tuple-element.15.refs_1_, f32[128,128]{1,0:T(8,128)S(1)} %get-tuple-element.16.refs_2_, ...), custom_call_target="tpu_custom_call" | custom-call | flops 4000000000 | bytes 18000000 | tf_op jit(solution)/shard_map/spread_first/pallas_call | solution.py:505
  68.6 4.7 %all-to-all-start.2 = ((bf16[128,2,8,512]{3,2,1,0:T(8,128)(2,1)}), bf16[128,2,8,512]{3,2,1,0:T(8,128)(2,1)S(1)}, u32[]{:S(2)}, u32[]{:S(2)}) async-start(bf16[128,2,8,512]{3,2,1,0:T(8,128)(2,1)} %bitcast.29), calls=%async_computation.2 | async-start | bytes 4194304 | tf_op jit(solution)/shard_map/all_to_all | solution.py:535
  73.3 0.1 collective-permute-start.2
  73.3 7.2 %collective-permute-start.3 = (bf16[128,512]{1,0:T(8,128)(2,1)S(1)}, bf16[128,512]{1,0:T(8,128)(2,1)S(1)}, u32[]{:S(2)}, u32[]{:S(2)}) collective-permute-start(bf16[128,512]{1,0:T(8,128)(2,1)S(1)} %bitcast.22), channel_id=1, source_target_pairs={{1,0},{2,1},{3,2},{4,3},{5,4},{6,5},{7,6},{8,7},{9,8},{10,9},{11,1... | collective-permute-start | bytes 393224 | tf_op jit(solution)/shard_map/ppermute | solution.py:521
  80.5 3.8 %change.1.refs_1_ = f32[1,128]{1,0:T(1,128)S(1)} custom-call(bf16[4096,512]{1,0:T(8,128)(2,1)} %bitcast.30, bf16[4096,512]{1,0:T(8,128)(2,1)} %old_hbm.1), custom_call_target="tpu_custom_call" | custom-call | flops 5000000000 | bytes 8000000 | tf_op jit(solution)/shard_map/change/pallas_call | solution.py:301
  84.3 20.5 %collective-permute-done.2.refs_3_ = bf16[128,512]{1,0:T(8,128)(2,1)S(1)} collective-permute-done((bf16[128,512]{1,0:T(8,128)(2,1)S(1)}, bf16[128,512]{1,0:T(8,128)(2,1)S(1)}, u32[]{:S(2)}, u32[]{:S(2)}) %collective-permute-start.2) | collective-permute-done | bytes 131104 | tf_op jit(solution)/shard_map/ppermute | solution.py:521
  104.8 0.0 collective-permute-done.3.refs_4_
  104.8 0.0 all-to-all-done.2
  104.8 6.3 %spread_last.1 = (bf16[512,8,512]{2,1,0:T(8,128)(2,1)}, f32[2,32]{1,0:T(2,128)}) custom-call(s32[896]{0:T(1024)} %get-tuple-element.14.refs_0_, f32[1,128]{1,0:T(1,128)S(1)} %change.1.refs_1_, f32[128,128]{1,0:T(8,128)S(1)} %get-tuple-element.16.refs_2_, bf16[128,512]{1,0:T(8,128)(2,1)S(1)} %collective-permute-done.2.refs_3_, ...), custom_call_target="tpu_custom_call" | custom-call | flops 4000000000 | bytes 18000000 | tf_op jit(solution)/shard_map/spread_last/pallas_call | solution.py:505
  (4 shorter events, 0.0 us)
Async XLA Ops:
  21.7 16.4 %copy-start = (bf16[1,128,2,8,128]{4,3,2,1,0:T(8,128)(2,1)S(1)}, bf16[1,128,2,8,128]{4,3,2,1,0:T(8,128)(2,1)}, u32[]{:S(2)}) copy-start(bf16[1,128,2,8,128]{4,3,2,1,0:T(8,128)(2,1)} %param.13) | copy-start | bytes 1572868
  21.7 16.4 %copy-start.1 = (s32[4096]{0:T(1024)S(1)}, s32[4096]{0:T(1024)}, u32[]{:S(2)}) copy-start(s32[4096]{0:T(1024)} %param.8) | copy-start | bytes 49156
  21.7 16.4 %copy-start.2 = (s32[1,128,2]{1,2,0:T(2,128)S(1)}, s32[1,128,2]{1,2,0:T(2,128)}, u32[]{:S(2)}) copy-start(s32[1,128,2]{1,2,0:T(2,128)} %param.11) | copy-start | bytes 3076
  21.7 16.4 %copy-start.3 = (s32[1,128]{1,0:T(1,128)S(1)}, s32[1,128]{1,0:T(1,128)}, u32[]{:S(2)}) copy-start(s32[1,128]{1,0:T(1,128)} %param.12) | copy-start | bytes 1540
  25.4 36.2 %all-to-all-start.1 = ((bf16[128,2,8,512]{3,2,1,0:T(8,128)(2,1)}), bf16[128,2,8,512]{3,2,1,0:T(8,128)(2,1)S(1)}, u32[]{:S(2)}, u32[]{:S(2)}) async-start(bf16[128,2,8,512]{3,2,1,0:T(8,128)(2,1)} %bitcast.28), calls=%async_computation.1 | async-start | bytes 4194304 | tf_op jit(solution)/shard_map/all_to_all | solution.py:535
  31.0 22.0 %collective-permute-start.1 = (bf16[128,512]{1,0:T(8,128)(2,1)S(1)}, bf16[128,512]{1,0:T(8,128)(2,1)S(1)}, u32[]{:S(2)}, u32[]{:S(2)}) collective-permute-start(bf16[128,512]{1,0:T(8,128)(2,1)S(1)} %get-tuple-element.26), channel_id=1, source_target_pairs={{1,0},{2,1},{3,2},{4,3},{5,4},{6,5},{7,6},{8,7},{9,8},{10,9},{11,1... | collective-permute-start | bytes 393224 | tf_op jit(solution)/shard_map/ppermute | solution.py:521
  38.1 23.5 %collective-permute-start = (bf16[128,512]{1,0:T(8,128)(2,1)S(1)}, bf16[128,512]{1,0:T(8,128)(2,1)S(1)}, u32[]{:S(2)}, u32[]{:S(2)}) collective-permute-start(bf16[128,512]{1,0:T(8,128)(2,1)S(1)} %get-tuple-element.27), channel_id=1, source_target_pairs={{0,1},{1,2},{2,3},{3,4},{4,5},{5,6},{6,7},{7,8},{8,9},{9,10},{10,1... | collective-permute-start | bytes 393224 | tf_op jit(solution)/shard_map/ppermute | solution.py:521
  68.6 36.2 %all-to-all-start.2 = ((bf16[128,2,8,512]{3,2,1,0:T(8,128)(2,1)}), bf16[128,2,8,512]{3,2,1,0:T(8,128)(2,1)S(1)}, u32[]{:S(2)}, u32[]{:S(2)}) async-start(bf16[128,2,8,512]{3,2,1,0:T(8,128)(2,1)} %bitcast.29), calls=%async_computation.2 | async-start | bytes 4194304 | tf_op jit(solution)/shard_map/all_to_all | solution.py:535
  73.3 31.5 %collective-permute-start.2 = (bf16[128,512]{1,0:T(8,128)(2,1)S(1)}, bf16[128,512]{1,0:T(8,128)(2,1)S(1)}, u32[]{:S(2)}, u32[]{:S(2)}) collective-permute-start(bf16[128,512]{1,0:T(8,128)(2,1)S(1)} %bitcast.23), channel_id=1, source_target_pairs={{0,1},{1,2},{2,3},{3,4},{4,5},{5,6},{6,7},{7,8},{8,9},{9,10},{10,1... | collective-permute-start | bytes 393224 | tf_op jit(solution)/shard_map/ppermute | solution.py:521
  73.3 31.5 %collective-permute-start.3 = (bf16[128,512]{1,0:T(8,128)(2,1)S(1)}, bf16[128,512]{1,0:T(8,128)(2,1)S(1)}, u32[]{:S(2)}, u32[]{:S(2)}) collective-permute-start(bf16[128,512]{1,0:T(8,128)(2,1)S(1)} %bitcast.22), channel_id=1, source_target_pairs={{1,0},{2,1},{3,2},{4,3},{5,4},{6,5},{7,6},{8,7},{9,8},{10,9},{11,1... | collective-permute-start | bytes 393224 | tf_op jit(solution)/shard_map/ppermute | solution.py:521

commit v4 on v3

--- a/solution.py
+++ b/solution.py
@@ -8,7 +8,7 @@
 ITERS = 2
 CAP = 16
 GROUP = 4
-AHEAD = 4
+AHEAD = 7
 UNROLL = 8
 F32 = jnp.float32
 BF16 = jnp.bfloat16
@@ -407,7 +407,7 @@
     def place(t):
         far_ref[t] = gathered(t)
 
-    loop(0, tiles, place, unroll=2)
+    loop(0, tiles, place, unroll=4)
     get_cur(0).wait()
 
     def ready(g):

time: 112 us -> 111 us (level)
  transfers between devices with their start and end apart: 6 -> 6, of which waited for: 3 -> 3; matrix products, arithmetic and copies ran while one was open for 1% -> 1% of each run, Pallas kernels for 12% -> 11%
where the time goes in v4:
time: 111 us
  waiting for transfers between devices  35 us (32%)
  Pallas kernels  29.3 us (26%)
  starting transfers between devices  23.7 us (21%)
  blocking collectives  20.3 us (18%)
  local copies, waits for them, and re-layouts  1.79 us (2%)
    ppermute x2, waiting for transfers between devices, halos(): lax.ppermute(last, 'node', forward)  29 us
    all_to_all x1, blocking collectives, body(): lax.all_to_all(far_block, 'node', split_axis=1, concat_axis=0, tiled=True)  20.3 us
    ppermute x2, starting transfers between devices, halos(): lax.ppermute(first, 'node', backward)  14.3 us
    pallas_call x2, Pallas kernels, spread_call(): pl.pallas_call(lambda *refs: spread_kernel(first, *refs), out_shape=outs,...  13.2 us
    all_to_all x2, starting transfers between devices, exchange(): lax.all_to_all(x, 'node', split_axis=0, concat_axis=0, tiled=True)  9.37 us
    pallas_call x1, Pallas kernels, prepare(): pl.pallas_call(prep_kernel, out_shape=(pltpu.HBM((table,), jnp.int32), ja...  8.95 us
    ppermute x2, waiting for transfers between devices, halos(): lax.ppermute(first, 'node', backward)  6 us
    pallas_call x1, Pallas kernels, change_sums(): pl.pallas_call(change_kernel, out_shape=jax.ShapeDtypeStruct((1, rows), F...  3.79 us
  transfers between devices with their start and end apart: 6, of which 3 were waited for; matrix products, arithmetic and copies ran while one was open for 1% of the time, Pallas kernels for 11%

profile of v4, /device:TPU:0, one launch (start us, length us, event | category | flops | bytes accessed | tf_op | source)
XLA Modules:
  0.0 110.8 jit_solution(12371632930108696263)
XLA Ops:
  0.6 0.8 copy.10
  1.4 20.3 %all_to_all.22 = s32[1,128,2]{2,0,1:T(1,128)S(1)} all-to-all(s32[1,128,2]{2,0,1:T(1,128)S(1)} %copy.10), channel_id=1, replica_groups=mesh['node'=128] {'node'}, dimensions={1} | all-to-all | bytes 2048 | tf_op jit(solution)/shard_map/all_to_all | solution.py:529
  21.7 3.5 %pick.1 = (s32[2,128]{1,0:T(2,128)}, bf16[16,16,8,512]{3,2,1,0:T(8,128)(2,1)}) custom-call(s32[128,1,2]{2,1,0:T(1,128)S(1)} %bitcast.20, bf16[512,8,512]{2,1,0:T(8,128)(2,1)} %bitcast.27), custom_call_target="tpu_custom_call" | custom-call | flops 1000000000 | bytes 4000000 | tf_op jit(solution)/shard_map/pick/pallas_call | solution.py:92
  25.2 4.7 %all-to-all-start.1 = ((bf16[128,2,8,512]{3,2,1,0:T(8,128)(2,1)}), bf16[128,2,8,512]{3,2,1,0:T(8,128)(2,1)S(1)}, u32[]{:S(2)}, u32[]{:S(2)}) async-start(bf16[128,2,8,512]{3,2,1,0:T(8,128)(2,1)} %bitcast.28), calls=%async_computation.1 | async-start | bytes 4194304 | tf_op jit(solution)/shard_map/all_to_all | solution.py:535
  29.9 1.0 fusion
  30.9 7.1 %collective-permute-start.1 = (bf16[128,512]{1,0:T(8,128)(2,1)S(1)}, bf16[128,512]{1,0:T(8,128)(2,1)S(1)}, u32[]{:S(2)}, u32[]{:S(2)}) collective-permute-start(bf16[128,512]{1,0:T(8,128)(2,1)S(1)} %get-tuple-element.26), channel_id=1, source_target_pairs={{1,0},{2,1},{3,2},{4,3},{5,4},{6,5},{7,6},{8,7},{9,8},{10,9},{11,1... | collective-permute-start | bytes 393224 | tf_op jit(solution)/shard_map/ppermute | solution.py:521
  38.0 0.0 collective-permute-start
  38.0 0.0 copy-done
  38.0 0.0 copy-done.1
  38.0 0.0 copy-done.2
  38.0 0.0 copy-done.3
  38.0 9.0 %prep.1 = (s32[896]{0:T(1024)}, f32[128,128]{1,0:T(8,128)S(1)}, bf16[32,128,512]{2,1,0:T(8,128)(2,1)}, bf16[16,128,128]{2,1,0:T(8,128)(2,1)}) custom-call(s32[256]{0:T(256)S(1)} %bitcast.25, s32[128]{0:T(128)S(1)} %bitcast.26, s32[32,1,128]{2,1,0:T(1,128)S(1)} %bitcast.24, bf16[256,8,128]{2,1,0:T(8,128)(2,1)S(1)} %bitcast.21, bf16[32,3,128,128]{3,2,1,0:T(8,128)(2,1)} %band_hbm.1), custom_call_target="tpu_custom_call" | custom-call | flops 10000000000 | bytes 16000000 | tf_op jit(solution)/shard_map/prep/pallas_call | solution.py:241
  47.0 6.0 %collective-permute-done.1.refs_4_ = bf16[128,512]{1,0:T(8,128)(2,1)S(1)} collective-permute-done((bf16[128,512]{1,0:T(8,128)(2,1)S(1)}, bf16[128,512]{1,0:T(8,128)(2,1)S(1)}, u32[]{:S(2)}, u32[]{:S(2)}) %collective-permute-start.1) | collective-permute-done | bytes 131104 | tf_op jit(solution)/shard_map/ppermute | solution.py:521
  53.0 8.5 %collective-permute-done.refs_3_ = bf16[128,512]{1,0:T(8,128)(2,1)S(1)} collective-permute-done((bf16[128,512]{1,0:T(8,128)(2,1)S(1)}, bf16[128,512]{1,0:T(8,128)(2,1)S(1)}, u32[]{:S(2)}, u32[]{:S(2)}) %collective-permute-start) | collective-permute-done | bytes 131104 | tf_op jit(solution)/shard_map/ppermute | solution.py:521
  61.5 0.0 all-to-all-done.1
  61.5 6.8 %spread_first.1 = (bf16[512,8,512]{2,1,0:T(8,128)(2,1)}, bf16[16,16,8,512]{3,2,1,0:T(8,128)(2,1)}, bf16[16,8,512]{2,1,0:T(8,128)(2,1)S(1)}, bf16[16,8,512]{2,1,0:T(8,128)(2,1)S(1)}) custom-call(s32[896]{0:T(1024)} %get-tuple-element.14.refs_0_, s32[2,128]{1,0:T(2,128)} %get-tuple-element.15.refs_1_, f32[128,128]{1,0:T(8,128)S(1)} %get-tuple-element.16.refs_2_, ...), custom_call_target="tpu_custom_call" | custom-call | flops 4000000000 | bytes 18000000 | tf_op jit(solution)/shard_map/spread_first/pallas_call | solution.py:505
  68.3 4.7 %all-to-all-start.2 = ((bf16[128,2,8,512]{3,2,1,0:T(8,128)(2,1)}), bf16[128,2,8,512]{3,2,1,0:T(8,128)(2,1)S(1)}, u32[]{:S(2)}, u32[]{:S(2)}) async-start(bf16[128,2,8,512]{3,2,1,0:T(8,128)(2,1)} %bitcast.29), calls=%async_computation.2 | async-start | bytes 4194304 | tf_op jit(solution)/shard_map/all_to_all | solution.py:535
  73.0 0.1 collective-permute-start.2
  73.0 7.2 %collective-permute-start.3 = (bf16[128,512]{1,0:T(8,128)(2,1)S(1)}, bf16[128,512]{1,0:T(8,128)(2,1)S(1)}, u32[]{:S(2)}, u32[]{:S(2)}) collective-permute-start(bf16[128,512]{1,0:T(8,128)(2,1)S(1)} %bitcast.22), channel_id=1, source_target_pairs={{1,0},{2,1},{3,2},{4,3},{5,4},{6,5},{7,6},{8,7},{9,8},{10,9},{11,1... | collective-permute-start | bytes 393224 | tf_op jit(solution)/shard_map/ppermute | solution.py:521
  80.2 3.8 %change.1.refs_1_ = f32[1,128]{1,0:T(1,128)S(1)} custom-call(bf16[4096,512]{1,0:T(8,128)(2,1)} %bitcast.30, bf16[4096,512]{1,0:T(8,128)(2,1)} %old_hbm.1), custom_call_target="tpu_custom_call" | custom-call | flops 5000000000 | bytes 8000000 | tf_op jit(solution)/shard_map/change/pallas_call | solution.py:301
  84.0 20.5 %collective-permute-done.2.refs_3_ = bf16[128,512]{1,0:T(8,128)(2,1)S(1)} collective-permute-done((bf16[128,512]{1,0:T(8,128)(2,1)S(1)}, bf16[128,512]{1,0:T(8,128)(2,1)S(1)}, u32[]{:S(2)}, u32[]{:S(2)}) %collective-permute-start.2) | collective-permute-done | bytes 131104 | tf_op jit(solution)/shard_map/ppermute | solution.py:521
  104.5 0.0 collective-permute-done.3.refs_4_
  104.5 0.0 all-to-all-done.2
  104.5 6.3 %spread_last.1 = (bf16[512,8,512]{2,1,0:T(8,128)(2,1)}, f32[2,32]{1,0:T(2,128)}) custom-call(s32[896]{0:T(1024)} %get-tuple-element.14.refs_0_, f32[1,128]{1,0:T(1,128)S(1)} %change.1.refs_1_, f32[128,128]{1,0:T(8,128)S(1)} %get-tuple-element.16.refs_2_, bf16[128,512]{1,0:T(8,128)(2,1)S(1)} %collective-permute-done.2.refs_3_, ...), custom_call_target="tpu_custom_call" | custom-call | flops 4000000000 | bytes 18000000 | tf_op jit(solution)/shard_map/spread_last/pallas_call | solution.py:505
  (4 shorter events, 0.0 us)
Async XLA Ops:
  21.7 16.3 %copy-start = (bf16[1,128,2,8,128]{4,3,2,1,0:T(8,128)(2,1)S(1)}, bf16[1,128,2,8,128]{4,3,2,1,0:T(8,128)(2,1)}, u32[]{:S(2)}) copy-start(bf16[1,128,2,8,128]{4,3,2,1,0:T(8,128)(2,1)} %param.13) | copy-start | bytes 1572868
  21.7 16.3 %copy-start.1 = (s32[4096]{0:T(1024)S(1)}, s32[4096]{0:T(1024)}, u32[]{:S(2)}) copy-start(s32[4096]{0:T(1024)} %param.8) | copy-start | bytes 49156
  21.7 16.3 %copy-start.2 = (s32[1,128,2]{1,2,0:T(2,128)S(1)}, s32[1,128,2]{1,2,0:T(2,128)}, u32[]{:S(2)}) copy-start(s32[1,128,2]{1,2,0:T(2,128)} %param.11) | copy-start | bytes 3076
  21.7 16.3 %copy-start.3 = (s32[1,128]{1,0:T(1,128)S(1)}, s32[1,128]{1,0:T(1,128)}, u32[]{:S(2)}) copy-start(s32[1,128]{1,0:T(1,128)} %param.12) | copy-start | bytes 1540
  25.2 36.3 %all-to-all-start.1 = ((bf16[128,2,8,512]{3,2,1,0:T(8,128)(2,1)}), bf16[128,2,8,512]{3,2,1,0:T(8,128)(2,1)S(1)}, u32[]{:S(2)}, u32[]{:S(2)}) async-start(bf16[128,2,8,512]{3,2,1,0:T(8,128)(2,1)} %bitcast.28), calls=%async_computation.1 | async-start | bytes 4194304 | tf_op jit(solution)/shard_map/all_to_all | solution.py:535
  30.9 22.1 %collective-permute-start.1 = (bf16[128,512]{1,0:T(8,128)(2,1)S(1)}, bf16[128,512]{1,0:T(8,128)(2,1)S(1)}, u32[]{:S(2)}, u32[]{:S(2)}) collective-permute-start(bf16[128,512]{1,0:T(8,128)(2,1)S(1)} %get-tuple-element.26), channel_id=1, source_target_pairs={{1,0},{2,1},{3,2},{4,3},{5,4},{6,5},{7,6},{8,7},{9,8},{10,9},{11,1... | collective-permute-start | bytes 393224 | tf_op jit(solution)/shard_map/ppermute | solution.py:521
  38.0 23.5 %collective-permute-start = (bf16[128,512]{1,0:T(8,128)(2,1)S(1)}, bf16[128,512]{1,0:T(8,128)(2,1)S(1)}, u32[]{:S(2)}, u32[]{:S(2)}) collective-permute-start(bf16[128,512]{1,0:T(8,128)(2,1)S(1)} %get-tuple-element.27), channel_id=1, source_target_pairs={{0,1},{1,2},{2,3},{3,4},{4,5},{5,6},{6,7},{7,8},{8,9},{9,10},{10,1... | collective-permute-start | bytes 393224 | tf_op jit(solution)/shard_map/ppermute | solution.py:521
  68.3 36.2 %all-to-all-start.2 = ((bf16[128,2,8,512]{3,2,1,0:T(8,128)(2,1)}), bf16[128,2,8,512]{3,2,1,0:T(8,128)(2,1)S(1)}, u32[]{:S(2)}, u32[]{:S(2)}) async-start(bf16[128,2,8,512]{3,2,1,0:T(8,128)(2,1)} %bitcast.29), calls=%async_computation.2 | async-start | bytes 4194304 | tf_op jit(solution)/shard_map/all_to_all | solution.py:535
  73.0 31.5 %collective-permute-start.2 = (bf16[128,512]{1,0:T(8,128)(2,1)S(1)}, bf16[128,512]{1,0:T(8,128)(2,1)S(1)}, u32[]{:S(2)}, u32[]{:S(2)}) collective-permute-start(bf16[128,512]{1,0:T(8,128)(2,1)S(1)} %bitcast.23), channel_id=1, source_target_pairs={{0,1},{1,2},{2,3},{3,4},{4,5},{5,6},{6,7},{7,8},{8,9},{9,10},{10,1... | collective-permute-start | bytes 393224 | tf_op jit(solution)/shard_map/ppermute | solution.py:521
  73.0 31.5 %collective-permute-start.3 = (bf16[128,512]{1,0:T(8,128)(2,1)S(1)}, bf16[128,512]{1,0:T(8,128)(2,1)S(1)}, u32[]{:S(2)}, u32[]{:S(2)}) collective-permute-start(bf16[128,512]{1,0:T(8,128)(2,1)S(1)} %bitcast.22), channel_id=1, source_target_pairs={{1,0},{2,1},{3,2},{4,3},{5,4},{6,5},{7,6},{8,7},{9,8},{10,9},{11,1... | collective-permute-start | bytes 393224 | tf_op jit(solution)/shard_map/ppermute | solution.py:521
